TPU v7x, 128 devices: a whole 4x4x4 slice. The times are simulated.
128 devices in a mesh: dom: 32 (over x, y, core), shift: 4 (over z).
Axes of the slice: x: 4, y: 4, z: 4, core: 2. Of those that a mesh axis runs over, the one named last changes fastest.
Arguments:
- sources: float32 [32, 128, 16, 128], P('shift', 'dom'), may hold values from -6 to 6
- kappa: float32 [128, 16, 128], P('dom'), may hold values from 0 to 2
- mass: float32 [128, 16, 128], P('dom'), may hold values from 0.25 to 4
- shift_table: float32 [64], replicated, may hold values from 0.5 to 4
- shift_ids: int32 [16], P('shift'), may hold values from 0 to 63
- sketch: bfloat16 [1024, 128, 16, 128], P(None, 'dom'), may hold values from -0.1875 to 0.1875
Outputs:
- solution: float32 [16, 32, 128, 16, 128], P('shift', None, 'dom')
- residual: float32 [16, 32, 128, 16, 128], P('shift', None, 'dom')
Inputs may be any that keep to these rules, and one draw needn't show every extreme that they name: `shift_ids`: index into shift_table.
All inputs are finite; a program needn't handle non-finite values.
Results may differ from a plain program's by a relative error of at most 0.0026.
Values sent between devices are 32-bit elements; how exact they have to be, the bound alone decides.
A program may use at most 128 MiB of HBM per device.

v0:
```python
import jax
import jax.numpy as jnp
from jax import lax
from jax.sharding import PartitionSpec as P


def sent_to_all(array, axis):
    copies = jnp.broadcast_to(array, (lax.axis_size(axis), *array.shape))
    return lax.all_to_all(copies, axis, split_axis=0, concat_axis=0, tiled=True)


def joined_along(pieces, dim):
    pieces = jnp.moveaxis(pieces, 0, dim)
    lengths = pieces.shape
    return pieces.reshape(*lengths[:dim], lengths[dim] * lengths[dim + 1], *lengths[dim + 2 :])


def gather_directly(array, axis, dim):
    pieces = sent_to_all(array, axis)
    return joined_along(pieces, dim)


def padded(block, sides, width):
    for axis, dim in sides:
        count = lax.axis_size(axis)
        forward = [(i, i + 1) for i in range(count - 1)]
        backward = [(target, source) for source, target in forward]
        low = lax.ppermute(
            lax.slice_in_dim(block, block.shape[dim] - width, None, axis=dim), axis, forward
        )
        high = lax.ppermute(lax.slice_in_dim(block, 0, width, axis=dim), axis, backward)
        block = jnp.concatenate([low, block, high], axis=dim)
    return block


def in_blocks(array, dim, count):
    lengths = array.shape
    pieces = array.reshape(*lengths[:dim], count, lengths[dim] // count, *lengths[dim + 1 :])
    return jnp.moveaxis(pieces, dim, 0)


def sent_and_summed(array, axis, dim):
    count = lax.axis_size(axis)
    pieces = lax.all_to_all(in_blocks(array, dim, count), axis, 0, 0, tiled=True)
    return jnp.sum(pieces, axis=0)


def taken_together(array, axis):
    everything = sent_to_all(array, axis)
    return jnp.sum(everything, axis=0)


def shift_values(shift_table, shift_ids):
    entries = jnp.arange(shift_table.shape[0], dtype=jnp.int32)
    picked = jnp.where(shift_ids[:, None] == entries[None, :], shift_table[None, :], 0.0)
    return jnp.sum(picked, axis=1)


def trimmed(field, diag_wide, valid, offset):
    inner = field[:, :, 1:-1]
    planes = inner.shape[2]
    beside = field[:, :, 2:] + field[:, :, :-2]
    sides = jnp.pad(inner, ((0, 0), (0, 0), (0, 0), (1, 1), (1, 1)))
    beside = beside + sides[:, :, :, 2:, 1:-1] + sides[:, :, :, :-2, 1:-1]
    beside = beside + sides[:, :, :, 1:-1, 2:] + sides[:, :, :, 1:-1, :-2]
    diag = diag_wide[:, :, offset : offset + planes]
    inside = valid[offset : offset + planes][None, None, :, None, None]
    return (diag * inner - beside) * inside


def solve_small(gram):
    h_vals = [gram[:, 1 + i, 0] for i in range(3)]
    ridge = 0.001 * (gram[:, 1, 1] + gram[:, 2, 2] + gram[:, 3, 3]) / 3.0 + 1.0
    entry = [
        [gram[:, 1 + i, 1 + k] + (ridge if i == k else 0.0) for k in range(3)] for i in range(3)
    ]
    l00 = jnp.sqrt(entry[0][0])
    l10 = entry[1][0] / l00
    l20 = entry[2][0] / l00
    l11 = jnp.sqrt(entry[1][1] - l10 * l10)
    l21 = (entry[2][1] - l20 * l10) / l11
    l22 = jnp.sqrt(entry[2][2] - l20 * l20 - l21 * l21)
    f0 = h_vals[0] / l00
    f1 = (h_vals[1] - l10 * f0) / l11
    f2 = (h_vals[2] - l20 * f0 - l21 * f1) / l22
    c2 = f2 / l22
    c1 = (f1 - l21 * c2) / l11
    c0 = (f0 - l10 * c1 - l20 * c2) / l00
    return (c0, c1, c2)


def gram_of(sketched):
    return jnp.einsum("rib,rkb->bik", sketched, sketched, precision=lax.Precision.HIGHEST)


def project(rows, fields):
    return lax.dot_general(
        rows, fields, (((1,), (1,)), ((), ())), preferred_element_type=jnp.float32
    )


def assemble(source_part, image_part, count):
    rows = source_part.shape[0]
    tiled = jnp.tile(source_part, (1, count))
    systems = tiled.shape[1]
    images = image_part.reshape(rows, 3, systems)
    return jnp.concatenate([tiled[:, None, :], images], axis=1)


def on_device(sources, kappa, mass, shift_table, shift_ids, sketch):
    all_sources = gather_directly(sources, "shift", 0)
    sigma = shift_values(shift_table, shift_ids)
    count = sigma.shape[0]
    sources_count = all_sources.shape[0]
    systems = count * sources_count
    slab = kappa.shape[0]
    center = (6.0 + sigma)[:, None, None, None, None]
    w0 = jnp.broadcast_to(all_sources[None], (count,) + all_sources.shape)
    coeffs = jnp.stack([kappa, mass], axis=0)
    wide_sources, wide_coeffs = (
        padded(all_sources, (("dom", 1),), 3),
        padded(coeffs, (("dom", 1),), 3),
    )
    planes = wide_sources.shape[1]
    first = lax.axis_index("dom") * slab - 3
    global_plane = first + jnp.arange(planes, dtype=jnp.int32)
    valid = ((global_plane >= 0) & (global_plane < slab * lax.axis_size("dom"))).astype(jnp.float32)
    diag_wide = (
        6.0
        - wide_coeffs[0][None, None]
        + sigma[:, None, None, None, None] * wide_coeffs[1][None, None]
    )
    padded_w0 = wide_sources[None]
    wide_z0 = trimmed(padded_w0, diag_wide, valid, 1)
    wide_w1 = (wide_z0 - center * padded_w0[:, :, 1:-1]) / 6.0
    wide_z1 = trimmed(wide_w1, diag_wide, valid, 2)
    wide_w2 = (wide_z1 - center * wide_w1[:, :, 1:-1]) / 6.0
    z2 = trimmed(wide_w2, diag_wide, valid, 3)
    z0 = wide_z0[:, :, 2:-2]
    w1 = wide_w1[:, :, 2:-2]
    z1 = wide_z1[:, :, 1:-1]
    w2 = wide_w2[:, :, 1:-1]
    matrix = sketch.reshape(sketch.shape[0], -1)
    source_flat = all_sources.astype(jnp.bfloat16).reshape(sources_count, -1)
    images = [z0, z1, z2]

    def flatten(field):
        return field.astype(jnp.bfloat16).reshape(systems, -1)

    stacked = jnp.concatenate([source_flat] + [flatten(field) for field in images], axis=0)
    owned = sent_and_summed(project(matrix, stacked), "dom", 0)
    local_gram = gram_of(assemble(owned[:, :sources_count], owned[:, sources_count:], count))
    gram = taken_together(local_gram, "dom")
    c0, c1, c2 = solve_small(gram)
    shape = (count, sources_count, 1, 1, 1)
    c0 = c0.reshape(shape)
    c1 = c1.reshape(shape)
    c2 = c2.reshape(shape)
    solution = c0 * w0 + c1 * w1 + c2 * w2
    residual = w0 - c0 * z0 - c1 * z1 - c2 * z2
    return (solution, residual)


def solution(mesh):
    placed = (
        P("shift", "dom", None, None),
        P("dom", None, None),
        P("dom", None, None),
        P(),
        P("shift"),
        P(None, "dom", None, None),
    )
    return jax.shard_map(
        on_device,
        mesh=mesh,
        in_specs=placed,
        out_specs=(P("shift", None, "dom", None, None), P("shift", None, "dom", None, None)),
        check_vma=False,
    )
```

profile of v0, /device:TPU:0, one launch (start us, length us, event | category | flops | bytes accessed | tf_op | source)
XLA Modules:
  0.0 177.7 jit_solution(3296555358565667610)
XLA Ops:
  2.8 5.4 %all-to-all-start = ((f32[4,8,4,16,128]{4,1,3,2,0:T(8,128)}), f32[4,8,4,16,128]{4,1,3,2,0:T(8,128)S(1)}, u32[]{:S(2)}, u32[]{:S(2)}) async-start(f32[4,8,4,16,128]{4,1,3,2,0:T(8,128)} %broadcast_in_dim.20), calls=%async_computation | async-start | bytes 2097152 | tf_op jit(solution)/shard_map/all_to_all | solution.py:9
  9.1 1.3 collective-permute-start.1
  10.4 3.0 %collective-permute-start = (f32[2,3,16,128]{3,2,1,0:T(8,128)S(1)}, f32[2,3,16,128]{3,2,1,0:T(8,128)S(1)}, u32[]{:S(2)}, u32[]{:S(2)}) collective-permute-start(f32[2,3,16,128]{3,2,1,0:T(8,128)S(1)} %get-tuple-element.30), channel_id=1, source_target_pairs={{0,4},{4,8},{8,12},{12,16},{16,20},{20,24},{24,28},{28,32},{32,36}... | collective-permute-start | bytes 147464 | tf_op jit(solution)/shard_map/ppermute | solution.py:28
  15.3 8.0 %all-to-all-done = f32[4,8,4,16,128]{4,1,3,2,0:T(8,128)S(1)} async-done(((f32[4,8,4,16,128]{4,1,3,2,0:T(8,128)}), f32[4,8,4,16,128]{4,1,3,2,0:T(8,128)S(1)}, u32[]{:S(2)}, u32[]{:S(2)}) %all-to-all-start) | async-done | bytes 1048608 | tf_op jit(solution)/shard_map/all_to_all | solution.py:9
  23.7 1.3 collective-permute-start.3
  25.0 3.1 %collective-permute-start.2 = (f32[32,3,16,128]{3,2,1,0:T(8,128)S(1)}, f32[32,3,16,128]{3,2,1,0:T(8,128)S(1)}, u32[]{:S(2)}, u32[]{:S(2)}) collective-permute-start(f32[32,3,16,128]{3,2,1,0:T(8,128)S(1)} %get-tuple-element.26), channel_id=1, source_target_pairs={{0,4},{4,8},{8,12},{12,16},{16,20},{20,24},{24,28},{28,32},{32,36}... | collective-permute-start | bytes 2359304 | tf_op jit(solution)/shard_map/ppermute | solution.py:28
  30.4 1.4 fusion.28
  31.8 4.3 %subtract_multiply_fusion.1 = (f32[4,32,8,16,128]{4,3,2,1,0:T(8,128)}, f32[4,32,8,16,128]{4,3,2,1,0:T(8,128)S(1)}) fusion(f32[8]{0:T(128)S(1)} %slice.161, f32[32,8,16,128]{3,2,1,0:T(8,128)S(1)} %get-tuple-element.22, f32[32,8,16,128]{3,2,1,0:T(8,128)S(1)} %get-tuple-element.23, f32[4,8,16,128]{3,2,1,0:T(8,128)S(1)} %slice_bitcast_fusion, ...), kind=kLoop, calls=%fused_computation.16 | loop fusion | flops 12582912 | bytes 21233712 | tf_op jit(solution)/shard_map/mul | solution.py:68
  36.1 3.2 %copy-done = f32[4,32,8,16,128]{4,3,2,1,0:T(8,128)} copy-done((f32[4,32,8,16,128]{4,3,2,1,0:T(8,128)}, f32[4,32,8,16,128]{4,3,2,1,0:T(8,128)S(1)}, u32[]{:S(2)}) %copy-start) | copy-done | bytes 8388632
  39.3 3.3 %slice.206 = f32[4,32,6,16,128]{4,3,2,1,0:T(8,128)} slice(f32[4,32,8,16,128]{4,3,2,1,0:T(8,128)S(1)} %get-tuple-element.21), slice={[0:4], [0:32], [1:7], [0:16], [0:128]} | slice | bytes 12582912 | tf_op jit(solution)/shard_map/slice | solution.py:60
  42.6 20.3 %subtract_multiply_fusion.2 = (f32[4,32,6,16,128]{4,3,2,1,0:T(8,128)S(1)}, f32[4,32,6,16,128]{4,3,2,1,0:T(8,128)}) fusion(f32[4]{0:T(128)S(1)} %broadcast_add_fusion, f32[4,32,8,16,128]{4,3,2,1,0:T(8,128)} %copy-done, f32[6]{0:T(128)S(1)} %slice.171, f32[4,32,6,16,128]{4,3,2,1,0:T(8,128)} %slice.206, f32[4,6,16,128]{3,2,1,0:T(8,128)S(1)} %slice_bitcast_fusion.1), kind=kLoop, calls=%fused_computation.31 | loop fusion | flops 17301504 | bytes 37945384 | tf_op jit(solution)/shard_map/div | solution.py:137
  63.4 2.2 %copy-done.1 = f32[4,32,6,16,128]{4,3,2,1,0:T(8,128)} copy-done((f32[4,32,6,16,128]{4,3,2,1,0:T(8,128)}, f32[4,32,6,16,128]{4,3,2,1,0:T(8,128)S(1)}, u32[]{:S(2)}) %copy-start.1) | copy-done | bytes 6291480
  65.6 4.7 %fusion.43 = (bf16[4,32,4,16,128]{4,3,2,1,0:T(8,128)(2,1)}, f32[4,32,4,16,128]{4,3,2,1,0:T(8,128)}) fusion(f32[4]{0:T(128)S(1)} %slice.181, f32[4,32,4,16,128]{4,3,2,1,0:T(8,128)S(1)} %slice.211, f32[4,32,6,16,128]{4,3,2,1,0:T(8,128)S(1)} %get-tuple-element.18, f32[4,4,16,128]{3,2,1,0:T(8,128)S(1)} %slice_bitcast_fusion.2), kind=kLoop, calls=%fused_computation.94 | loop fusion | flops 9437184 | bytes 19005456 | tf_op jit(solution)/shard_map/convert_element_type | solution.py:148
  70.3 4.2 %reshape.224 = bf16[128,8192]{1,0:T(8,128)(2,1)} reshape(bf16[4,32,4,16,128]{4,3,2,1,0:T(8,128)(2,1)} %get-tuple-element.16) | data formatting | bytes 4194304 | tf_op jit(solution)/shard_map/reshape | solution.py:148
  74.5 2.7 %slice.336 = bf16[4,32,4,16,128]{4,3,2,1,0:T(8,128)(2,1)S(1)} slice(f32[4,32,6,16,128]{4,3,2,1,0:T(8,128)} %get-tuple-element.19), slice={[0:4], [0:32], [1:5], [0:16], [0:128]} | slice | bytes 4194304 | tf_op jit(solution)/shard_map/slice | solution.py:141
  77.2 2.3 %reshape.223 = bf16[128,8192]{1,0:T(8,128)(2,1)} reshape(bf16[4,32,4,16,128]{4,3,2,1,0:T(8,128)(2,1)S(1)} %slice.336) | data formatting | bytes 4194304 | tf_op jit(solution)/shard_map/reshape | solution.py:148
  79.5 2.8 %slice.337 = bf16[4,32,4,16,128]{4,3,2,1,0:T(8,128)(2,1)S(1)} slice(f32[4,32,8,16,128]{4,3,2,1,0:T(8,128)} %get-tuple-element.20), slice={[0:4], [0:32], [2:6], [0:16], [0:128]} | slice | bytes 4194304 | tf_op jit(solution)/shard_map/slice | solution.py:139
  82.3 2.3 %reshape.222 = bf16[128,8192]{1,0:T(8,128)(2,1)} reshape(bf16[4,32,4,16,128]{4,3,2,1,0:T(8,128)(2,1)S(1)} %slice.337) | data formatting | bytes 4194304 | tf_op jit(solution)/shard_map/reshape | solution.py:148
  84.6 17.5 %fusion.29 = f32[1024,416]{0,1:T(8,128)} fusion(bf16[128,8,64,128]{3,2,1,0:T(8,128)(2,1)} %bitcast.47, bf16[128,8192]{1,0:T(8,128)(2,1)} %reshape.224, bf16[128,8192]{1,0:T(8,128)(2,1)} %reshape.223, bf16[128,8192]{1,0:T(8,128)(2,1)} %reshape.222, bf16[32,8192]{1,0:T(8,128)(2,1)S(1)} %bitcast.41), kind=kOutput, calls=%fused_computation.52 | convolution fusion | flops 7006584832 | bytes 25296896 | tf_op jit(solution)/shard_map/dot_general | solution.py:97
  102.1 1.9 %copy.24 = f32[1024,416]{1,0:T(8,128)S(1)} copy(f32[1024,416]{0,1:T(8,128)} %fusion.29) | data formatting | bytes 3407872 | tf_op jit(solution)/shard_map/dot_general | solution.py:97
  103.9 45.2 %all_to_all.15 = f32[32,32,416]{2,1,0:T(8,128)} all-to-all(f32[32,32,416]{2,1,0:T(8,128)S(1)} %bitcast.40), channel_id=1, replica_groups=mesh['dom'=32,'shift'=4] {'dom'}, dimensions={0} | all-to-all | bytes 3407872 | tf_op jit(solution)/shard_map/all_to_all | solution.py:44
  149.1 1.7 reduce_sum.28
  152.4 12.8 %all_to_all.16 = f32[32,128,4,4]{1,3,2,0:T(4,128)S(1)} all-to-all(f32[32,128,4,4]{1,3,2,0:T(4,128)S(1)} %broadcast_in_dim.38), channel_id=1, replica_groups=mesh['dom'=32,'shift'=4] {'dom'}, dimensions={0} | all-to-all | bytes 524288 | tf_op jit(solution)/shard_map/all_to_all | solution.py:9
  166.1 11.6 %multiply_subtract_fusion = (f32[4,32,4,16,128]{4,3,2,1,0:T(8,128)}, f32[4,32,4,16,128]{4,3,2,1,0:T(8,128)}) fusion(f32[4,32,4,16,128]{4,3,2,1,0:T(8,128)} %get-tuple-element.17, f32[4,32,6,16,128]{4,3,2,1,0:T(8,128)} %get-tuple-element.19, f32[4,32,8,16,128]{4,3,2,1,0:T(8,128)} %get-tuple-element.20, f32[4,32]{1,0:T(4,128)S(1)} %get-tuple-element.13, ...), kind=kLoop, calls=%fused_computation.42 | loop fusion | flops 11534336 | bytes 30410240 | tf_op jit(solution)/shard_map/sub | solution.py:160
  (56 shorter events, 10.4 us)
Async XLA Ops:
  2.8 20.5 %all-to-all-start = ((f32[4,8,4,16,128]{4,1,3,2,0:T(8,128)}), f32[4,8,4,16,128]{4,1,3,2,0:T(8,128)S(1)}, u32[]{:S(2)}, u32[]{:S(2)}) async-start(f32[4,8,4,16,128]{4,1,3,2,0:T(8,128)} %broadcast_in_dim.20), calls=%async_computation | async-start | bytes 2097152 | tf_op jit(solution)/shard_map/all_to_all | solution.py:9
  9.1 5.4 %collective-permute-start.1 = (f32[2,3,16,128]{3,2,1,0:T(8,128)S(1)}, f32[2,3,16,128]{3,2,1,0:T(8,128)S(1)}, u32[]{:S(2)}, u32[]{:S(2)}) collective-permute-start(f32[2,3,16,128]{3,2,1,0:T(8,128)S(1)} %get-tuple-element.31), channel_id=1, source_target_pairs={{4,0},{8,4},{12,8},{16,12},{20,16},{24,20},{28,24},{32,28},{36,32}... | collective-permute-start | bytes 147464 | tf_op jit(solution)/shard_map/ppermute | solution.py:31
  10.4 4.1 %collective-permute-start = (f32[2,3,16,128]{3,2,1,0:T(8,128)S(1)}, f32[2,3,16,128]{3,2,1,0:T(8,128)S(1)}, u32[]{:S(2)}, u32[]{:S(2)}) collective-permute-start(f32[2,3,16,128]{3,2,1,0:T(8,128)S(1)} %get-tuple-element.30), channel_id=1, source_target_pairs={{0,4},{4,8},{8,12},{12,16},{16,20},{20,24},{24,28},{28,32},{32,36}... | collective-permute-start | bytes 147464 | tf_op jit(solution)/shard_map/ppermute | solution.py:28
  23.5 6.7 %copy-start.2 = (f32[4,8,4,16,128]{4,3,2,1,0:T(8,128)}, f32[4,8,4,16,128]{4,3,2,1,0:T(8,128)S(1)}, u32[]{:S(2)}) copy-start(f32[4,8,4,16,128]{4,3,2,1,0:T(8,128)S(1)} %copy.23) | copy-start | bytes 3145732
  23.7 5.5 %collective-permute-start.3 = (f32[32,3,16,128]{3,2,1,0:T(8,128)S(1)}, f32[32,3,16,128]{3,2,1,0:T(8,128)S(1)}, u32[]{:S(2)}, u32[]{:S(2)}) collective-permute-start(f32[32,3,16,128]{3,2,1,0:T(8,128)S(1)} %get-tuple-element.27), channel_id=1, source_target_pairs={{4,0},{8,4},{12,8},{16,12},{20,16},{24,20},{28,24},{32,28},{36,32}... | collective-permute-start | bytes 2359304 | tf_op jit(solution)/shard_map/ppermute | solution.py:31
  25.0 4.9 %collective-permute-start.2 = (f32[32,3,16,128]{3,2,1,0:T(8,128)S(1)}, f32[32,3,16,128]{3,2,1,0:T(8,128)S(1)}, u32[]{:S(2)}, u32[]{:S(2)}) collective-permute-start(f32[32,3,16,128]{3,2,1,0:T(8,128)S(1)} %get-tuple-element.26), channel_id=1, source_target_pairs={{0,4},{4,8},{8,12},{12,16},{16,20},{20,24},{24,28},{28,32},{32,36}... | collective-permute-start | bytes 2359304 | tf_op jit(solution)/shard_map/ppermute | solution.py:28
  36.1 3.2 %copy-start = (f32[4,32,8,16,128]{4,3,2,1,0:T(8,128)}, f32[4,32,8,16,128]{4,3,2,1,0:T(8,128)S(1)}, u32[]{:S(2)}) copy-start(f32[4,32,8,16,128]{4,3,2,1,0:T(8,128)S(1)} %get-tuple-element.21) | copy-start | bytes 25165828
  62.9 2.7 %copy-start.1 = (f32[4,32,6,16,128]{4,3,2,1,0:T(8,128)}, f32[4,32,6,16,128]{4,3,2,1,0:T(8,128)S(1)}, u32[]{:S(2)}) copy-start(f32[4,32,6,16,128]{4,3,2,1,0:T(8,128)S(1)} %get-tuple-element.18) | copy-start | bytes 18874372
  79.5 5.1 %copy-start.4 = (bf16[4,8,4,16,128]{4,1,3,2,0:T(8,128)(2,1)S(1)}, bf16[4,8,4,16,128]{4,1,3,2,0:T(8,128)(2,1)}, u32[]{:S(2)}) copy-start(bf16[4,8,4,16,128]{4,1,3,2,0:T(8,128)(2,1)} %convert_element_type.25) | copy-start | bytes 1572868
  103.9 62.2 %copy-start.3 = (f32[4,8,4,16,128]{4,3,2,1,0:T(8,128)S(1)}, f32[4,8,4,16,128]{4,3,2,1,0:T(8,128)}, u32[]{:S(2)}) copy-start(f32[4,8,4,16,128]{4,3,2,1,0:T(8,128)} %copy-done.2) | copy-start | bytes 3145732
where the time goes:
time: 180 us; the launch traced here: 178 us
  blocking collectives  57.9 us (32%)
  other arithmetic  48 us (27%)
  local copies, waits for them, and re-layouts  29.5 us (16%)
  matrix products  18.5 us (10%)
  starting transfers between devices  14.1 us (8%)
  waiting for transfers between devices  8.8 us (5%)
    all_to_all x1, blocking collectives, sent_and_summed(): lax.all_to_all(in_blocks(array, dim, count), axis, 0, 0, tiled=True)  45.2 us
    div x1, other arithmetic, on_device(): wide_w2 = (wide_z1 - center * wide_w1[:, :, 1:-1]) / 6.0  20.3 us
    dot_general x1, matrix products, project(): lax.dot_general(rows, fields, (((1,), (1,)), ((), ())), preferred_element...  17.5 us
    all_to_all x1, blocking collectives, sent_to_all(): return lax.all_to_all(copies, axis, split_axis=0, concat_axis=0, tiled=True)  12.8 us
    sub x1, other arithmetic, on_device(): residual = w0 - c0 * z0 - c1 * z1 - c2 * z2  11.6 us
    reshape x3, local copies, waits for them, and re-layouts, flatten(): return field.astype(jnp.bfloat16).reshape(systems, -1)  8.8 us
    all_to_all x1, waiting for transfers between devices, sent_to_all(): return lax.all_to_all(copies, axis, split_axis=0, concat_axis=0, tiled=True)  8.01 us
    unnamed x11, local copies, waits for them, and re-layouts  6.53 us
  transfers between devices with their start and end apart: 5, of which 2 were waited for; matrix products, arithmetic and copies ran while one was open for 2% of the time, Pallas kernels for 0%

commit v1 on v0

v1 whole, which is shorter than its diff:
```python
import functools
import jax
import jax.numpy as jnp
from jax import lax
from jax.experimental import pallas as pl
from jax.experimental.pallas import tpu as pltpu
from jax.sharding import PartitionSpec as P

F32 = jnp.float32
BF16 = jnp.bfloat16
CENTER = 2.25
K0 = 6.0 + CENTER
LOW = (0, 1, 3, 4, 6, 7)
VMEM = pltpu.VMEM
ANY = pl.ANY
MiB = 1024 * 1024


def rdma(src, dst, send, recv, where):
    return pltpu.make_async_remote_copy(
        src_ref=src, dst_ref=dst, send_sem=send, recv_sem=recv,
        device_id=where, device_id_type=pl.DeviceIdType.MESH,
    )


def signal(sem, where):
    pl.semaphore_signal(sem, inc=1, device_id=where, device_id_type=pl.DeviceIdType.MESH)


def spread_kernel(doms, zs, src, kap, mas, wide, cw, loc, hs, hr, cs, cr, gs, gr):
    d, z = lax.axis_index("dom"), lax.axis_index("shift")
    up, down, far = lax.rem(z + 1, zs), lax.rem(z + zs - 1, zs), lax.rem(z + 2, zs)
    has_l, has_r = d > 0, d < doms - 1
    copies = [
        pltpu.make_async_copy(src, wide.at[z, :, pl.ds(3, 4)], loc.at[0]),
        pltpu.make_async_copy(kap, cw.at[0, pl.ds(2, 4)], loc.at[1]),
        pltpu.make_async_copy(mas, cw.at[1, pl.ds(2, 4)], loc.at[2]),
    ]
    for c in copies:
        c.start()
    bar = pltpu.get_barrier_semaphore()
    signal(bar, {"shift": up})
    signal(bar, {"shift": down})

    @pl.when(has_l)
    def _():
        signal(bar, {"dom": d - 1})

    @pl.when(has_r)
    def _():
        signal(bar, {"dom": d + 1})

    pl.semaphore_wait(bar, 2 + has_l.astype(jnp.int32) + has_r.astype(jnp.int32))

    @pl.when(d == 0)
    def _():
        for g in range(4):
            for s in range(8):
                wide[g, s, 0:3] = jnp.zeros((3, 16, 128), F32)
        cw[:, 0:2] = jnp.zeros((2, 2, 16, 128), F32)

    @pl.when(d == doms - 1)
    def _():
        for g in range(4):
            for s in range(8):
                wide[g, s, 7:10] = jnp.zeros((3, 16, 128), F32)
        cw[:, 6:8] = jnp.zeros((2, 2, 16, 128), F32)

    for c in copies:
        c.wait()

    def to_left(g):
        return rdma(wide.at[g, :, pl.ds(3, 3)], wide.at[g, :, pl.ds(7, 3)], hs.at[0, g], hr.at[0, g], {"dom": d - 1})

    def to_right(g):
        return rdma(wide.at[g, :, pl.ds(4, 3)], wide.at[g, :, pl.ds(0, 3)], hs.at[1, g], hr.at[1, g], {"dom": d + 1})

    def coeff_left():
        return rdma(cw.at[:, pl.ds(2, 2)], cw.at[:, pl.ds(6, 2)], cs.at[0], cr.at[0], {"dom": d - 1})

    def coeff_right():
        return rdma(cw.at[:, pl.ds(4, 2)], cw.at[:, pl.ds(0, 2)], cs.at[1], cr.at[1], {"dom": d + 1})

    def start_halo(g):
        @pl.when(has_l)
        def _():
            to_left(g).start()

        @pl.when(has_r)
        def _():
            to_right(g).start()

    @pl.when(has_l)
    def _():
        coeff_left().start()

    @pl.when(has_r)
    def _():
        coeff_right().start()

    start_halo(z)
    own = wide.at[z, :, pl.ds(3, 4)]
    send_up = rdma(own, own, gs.at[0], gr.at[0], {"shift": up})
    send_down = rdma(own, own, gs.at[1], gr.at[1], {"shift": down})
    send_up.start()
    send_down.start()
    send_up.wait_recv()
    half_a = wide.at[down, pl.ds(0, 4), pl.ds(3, 4)]
    relay_up = rdma(half_a, half_a, gs.at[2], gr.at[2], {"shift": up})
    relay_up.start()
    start_halo(down)
    send_down.wait_recv()
    half_b = wide.at[up, pl.ds(4, 4), pl.ds(3, 4)]
    relay_down = rdma(half_b, half_b, gs.at[3], gr.at[3], {"shift": down})
    relay_down.start()
    start_halo(up)
    relay_up.wait_recv()
    relay_down.wait_recv()
    start_halo(far)

    @pl.when(has_l)
    def _():
        coeff_left().wait_send()
        coeff_right().wait_recv()
        for g in range(4):
            to_left(g).wait_send()
            to_right(g).wait_recv()

    @pl.when(has_r)
    def _():
        coeff_right().wait_send()
        coeff_left().wait_recv()
        for g in range(4):
            to_right(g).wait_send()
            to_left(g).wait_recv()

    for c in (send_up, send_down, relay_up, relay_down):
        c.wait_send()


def neighbours(planes, i, masks):
    v = planes[i]
    first_y, last_y, first_z, last_z = masks
    beside = planes[i + 1] + planes[i - 1]
    beside = beside + jnp.where(first_y, 0.0, pltpu.roll(v, 1, 0)) + jnp.where(last_y, 0.0, pltpu.roll(v, 15, 0))
    return beside + jnp.where(first_z, 0.0, pltpu.roll(v, 1, 1)) + jnp.where(last_z, 0.0, pltpu.roll(v, 127, 1))


def make_masks():
    rows = lax.broadcasted_iota(jnp.int32, (16, 128), 0)
    lanes = lax.broadcasted_iota(jnp.int32, (16, 128), 1)
    return rows == 0, rows == 15, lanes == 0, lanes == 127


def fields_of(w, kap, mas, inside, masks):
    sixth = 1.0 / 6.0
    diag = [6.0 - kap[i] + CENTER * mas[i] for i in range(8)]

    def op(planes, i, k):
        return diag[k] * planes[i] - neighbours(planes, i, masks)

    z00, z01, p0, p1 = [], [], [], []
    for i in range(8):
        a = op(w, i + 1, i)
        b = mas[i] * w[i + 1]
        z00.append(a)
        z01.append(b)
        p0.append((a - K0 * w[i + 1]) * (sixth * inside[i]))
        p1.append((b - w[i + 1]) * sixth)
    z10, z11, z12, q0, q1, q2 = [], [], [], [], [], []
    for i in range(6):
        k = i + 1
        a = op(p0, k, k)
        b = op(p1, k, k) + mas[k] * p0[k]
        c = mas[k] * p1[k]
        z10.append(a)
        z11.append(b)
        z12.append(c)
        q0.append((a - K0 * p0[k]) * (sixth * inside[k]))
        q1.append((b - K0 * p1[k] - p0[k]) * (sixth * inside[k]))
        q2.append((c - p1[k]) * sixth)
    z20, z21, z22, z23 = [], [], [], []
    for i in range(4):
        k, n = i + 2, i + 1
        z20.append(op(q0, n, k))
        z21.append(op(q1, n, k) + mas[k] * q0[n])
        z22.append(op(q2, n, k) + mas[k] * q1[n])
        z23.append(mas[k] * q2[n])
    zs = [w[3:7], z00[2:6], z01[2:6], z10[1:5], z11[1:5], z12[1:5], z20, z21, z22, z23]
    ws = [p0[2:6], p1[2:6], q0[1:5], q1[1:5], q2[1:5]]
    return zs, ws


def inside_of(d, doms):
    out = []
    for i in range(8):
        plane = d * 4 + (i - 2)
        ok = (plane >= 0) & (plane < doms * 4)
        out.append(jnp.where(ok, 1.0, 0.0).astype(F32))
    return out


def sketch_kernel(doms, s_ref, wide, cw, out, buf, wb, cb, gb, ob, sems, loc):
    d, z = lax.axis_index("dom"), lax.axis_index("shift")
    pairs = [pltpu.make_async_copy(s_ref.at[:, q], buf.at[q], sems.at[q]) for q in range(32)]
    ins = [
        pltpu.make_async_copy(wide.at[z], wb, loc.at[0]),
        pltpu.make_async_copy(cw, cb, loc.at[1]),
    ]
    for c in ins:
        c.start()
    for c in pairs:
        c.start()
    for c in ins:
        c.wait()
    masks = make_masks()
    inside = inside_of(d, doms)
    kap = [cb[0, i] for i in range(8)]
    mas = [cb[1, i] for i in range(8)]

    def one(s, carry):
        w = [wb[s, i] for i in range(10)]
        zs, _ = fields_of(w, kap, mas, inside, masks)
        col = pl.multiple_of(s * 16, 16)
        for x in range(4):
            high = [f[x] for f in zs]
            low = [high[k] - high[k].astype(BF16).astype(F32) for k in LOW]
            stacked = jnp.stack(high + low, axis=0)
            turned = jnp.transpose(stacked, (1, 0, 2)).astype(BF16)
            for y in range(16):
                gb[x * 8 + y // 2, pl.ds((y % 2) * 128 + col, 16), :] = turned[y]
        return carry

    lax.fori_loop(0, 8, one, 0)
    for c in pairs:
        c.wait()
    rows = buf.reshape(32, 2048, 128)

    def block(i, carry):
        at = pl.multiple_of(i * 512, 512)
        lhs = jnp.concatenate([rows[q, pl.ds(at, 512), :] for q in range(32)], axis=1)
        rhs = jnp.concatenate([gb[q] for q in range(32)], axis=1)
        ob[pl.ds(at, 512), :] = lax.dot_general(lhs, rhs, (((1,), (1,)), ((), ())), preferred_element_type=F32)
        return carry

    lax.fori_loop(0, 4, block, 0)
    even = lax.broadcasted_iota(jnp.int32, (128, 128), 0) % 2 == 0
    for i in range(8):
        a = ob[128 * i : 128 * i + 128, :]
        b = ob[1024 + 128 * i : 1024 + 128 * i + 128, :]
        xa = a[:, :128] + pltpu.roll(a[:, 128:], 127, 0)
        xb = b[:, 128:] + pltpu.roll(b[:, :128], 1, 0)
        out[128 * i : 128 * i + 128, :] = jnp.where(even, xa, xb)


def gram_kernel(doms, zs, part, gall, r1, mine, r2, dm, rd, s1, e1, s2, e2, s3, e3, s4, e4):
    d, z = lax.axis_index("dom"), lax.axis_index("shift")
    core, chip, chips = lax.rem(d, 2), d // 2, doms // 2
    bar = pltpu.get_barrier_semaphore()
    for k in range(1, doms):
        signal(bar, {"dom": lax.rem(d + k, doms)})
    for k in range(1, zs):
        signal(bar, {"shift": lax.rem(z + k, zs)})
    pl.semaphore_wait(bar, doms + zs - 2)
    other = pl.multiple_of((1 - core) * 512, 512)
    keep = pl.multiple_of(core * 512, 512)
    swap = rdma(part.at[pl.ds(other, 512)], r1, s1, e1, {"dom": d + 1 - 2 * core})
    swap.start()
    swap.wait_recv()
    mine[...] = part[pl.ds(keep, 512)] + r1[...]
    sends = []
    for k in range(1, chips):
        t = lax.rem(chip + k, chips)
        c = rdma(mine.at[pl.ds(pl.multiple_of(t * 32, 32), 32)], r2.at[k], s2.at[k], e2.at[k], {"dom": 2 * t + core})
        c.start()
        sends.append(c)
    v = mine[pl.ds(pl.multiple_of(chip * 32, 32), 32)]
    for c, k in zip(sends, range(1, chips)):
        c.wait_recv()
        v = v + r2[k]
    full = lax.dot_general(v, v, (((0,), (0,)), ((), ())), precision=lax.Precision.HIGHEST, preferred_element_type=F32)
    owner = lax.broadcasted_iota(jnp.int32, (16, 128), 1) // 16
    diag = jnp.zeros((16, 128), F32)
    for s in range(8):
        diag = jnp.where(owner == s, full[16 * s : 16 * s + 16], diag)
    dm[...] = diag
    for k in range(1, doms):
        c = rdma(dm, rd.at[k], s3.at[k], e3.at[k], {"dom": lax.rem(d + k, doms)})
        c.start()
        sends.append(c)
    total = diag
    for k in range(1, doms):
        sends[chips - 2 + k].wait_recv()
        total = total + rd[k]
    gall[z] = total
    tail = []
    for k in range(1, zs):
        c = rdma(gall.at[z], gall.at[z], s4.at[k], e4.at[k], {"shift": lax.rem(z + k, zs)})
        c.start()
        tail.append(c)
    for c in tail:
        c.wait_recv()
    swap.wait_send()
    for c in sends + tail:
        c.wait_send()


def output_kernel(doms, step, coef, wide, cw, sol, res, fb):
    d = lax.axis_index("dom")
    base = pl.program_id(0) * step
    masks = make_masks()
    inside = inside_of(d, doms)
    kap = [cw[0, i] for i in range(8)]
    mas = [cw[1, i] for i in range(8)]

    def one(b, carry):
        w = [wide[b, i] for i in range(10)]
        zf, wf = fields_of(w, kap, mas, inside, masks)
        for n, f in enumerate(zf + wf):
            for x in range(4):
                fb[n, x] = f[x]

        def system(j, carry):
            at = (j * 32 + base + b) * 16
            c = [coef[at + i] for i in range(15)]
            for x in range(4):
                s = c[9] * fb[0, x]
                for n in range(10, 15):
                    s = s + c[n] * fb[n, x]
                r = fb[0, x]
                for n in range(9):
                    r = r - c[n] * fb[n + 1, x]
                sol[j, b, x] = s
                res[j, b, x] = r
            return carry

        lax.fori_loop(0, 4, system, 0)
        return carry

    lax.fori_loop(0, step, one, 0)


def shift_values(shift_table, shift_ids):
    entries = jnp.arange(shift_table.shape[0], dtype=jnp.int32)
    picked = jnp.where(shift_ids[:, None] == entries[None, :], shift_table[None, :], 0.0)
    return jnp.sum(picked, axis=1)


def solve_small(gram):
    h_vals = [gram[..., 1 + i, 0] for i in range(3)]
    ridge = 0.001 * (gram[..., 1, 1] + gram[..., 2, 2] + gram[..., 3, 3]) / 3.0 + 1.0
    entry = [[gram[..., 1 + i, 1 + k] + (ridge if i == k else 0.0) for k in range(3)] for i in range(3)]
    l00 = jnp.sqrt(entry[0][0])
    l10 = entry[1][0] / l00
    l20 = entry[2][0] / l00
    l11 = jnp.sqrt(entry[1][1] - l10 * l10)
    l21 = (entry[2][1] - l20 * l10) / l11
    l22 = jnp.sqrt(entry[2][2] - l20 * l20 - l21 * l21)
    f0 = h_vals[0] / l00
    f1 = (h_vals[1] - l10 * f0) / l11
    f2 = (h_vals[2] - l20 * f0 - l21 * f1) / l22
    c2 = f2 / l22
    c1 = (f1 - l21 * c2) / l11
    c0 = (f0 - l10 * c1 - l20 * c2) / l00
    return c0, c1, c2


def coefficients(gall, sigma):
    t = sigma - CENTER
    one, zero = jnp.ones_like(t), jnp.zeros_like(t)
    powers = [one, t, t * t, t * t * t]
    owner = [0, 1, 1, 2, 2, 2, 3, 3, 3, 3]
    degree = [0, 0, 1, 0, 1, 2, 0, 1, 2, 3]
    owner += [owner[k] for k in LOW]
    degree += [degree[k] for k in LOW]
    mix = jnp.stack(
        [jnp.stack([powers[degree[f]] if owner[f] == i else zero for f in range(16)], 1) for i in range(4)], 1
    )
    grams = gall.reshape(4, 16, 8, 16).transpose(0, 2, 1, 3).reshape(32, 16, 16)
    left = jnp.einsum("jif,bfg->jbig", mix, grams, precision=lax.Precision.HIGHEST)
    gram = jnp.einsum("jbig,jkg->jbik", left, mix, precision=lax.Precision.HIGHEST)
    c0, c1, c2 = solve_small(gram)
    t = t[:, None]
    out = [c0, c0 * t, c1, c1 * t, c1 * t * t, c2, c2 * t, c2 * t * t, c2 * t * t * t]
    out += [c0, c1, c1 * t, c2, c2 * t, c2 * t * t, jnp.zeros_like(c0)]
    return jnp.stack(out, axis=-1).reshape(-1)


def on_device(sources, kappa, mass, shift_table, shift_ids, sketch):
    doms, zs = lax.axis_size("dom"), lax.axis_size("shift")
    sds = jax.ShapeDtypeStruct
    dma = pltpu.SemaphoreType.DMA
    wide, cw = pl.pallas_call(
        functools.partial(spread_kernel, doms, zs),
        out_shape=(sds((4, 8, 10, 16, 128), F32), sds((2, 8, 16, 128), F32)),
        in_specs=[pl.BlockSpec(memory_space=ANY)] * 3,
        out_specs=(pl.BlockSpec(memory_space=VMEM), pl.BlockSpec(memory_space=VMEM)),
        scratch_shapes=[dma((3,)), dma((2, 4)), dma((2, 4)), dma((2,)), dma((2,)), dma((4,)), dma((4,))],
        compiler_params=pltpu.CompilerParams(collective_id=0, has_side_effects=True),
        name="spread",
    )(sources, kappa, mass)
    part = pl.pallas_call(
        functools.partial(sketch_kernel, doms),
        out_shape=sds((1024, 128), F32),
        in_specs=[pl.BlockSpec(memory_space=ANY)] * 3,
        out_specs=pl.BlockSpec(memory_space=VMEM),
        scratch_shapes=[
            VMEM((32, 1024, 2, 128), BF16), VMEM((8, 10, 16, 128), F32), VMEM((2, 8, 16, 128), F32),
            VMEM((32, 256, 128), BF16), VMEM((2048, 256), F32), dma((32,)), dma((2,)),
        ],
        compiler_params=pltpu.CompilerParams(vmem_limit_bytes=48 * MiB),
        name="sketch",
    )(sketch.reshape(1024, 32, 2, 128), wide, cw)
    gall = pl.pallas_call(
        functools.partial(gram_kernel, doms, zs),
        out_shape=sds((4, 16, 128), F32),
        in_specs=[pl.BlockSpec(memory_space=VMEM)],
        out_specs=pl.BlockSpec(memory_space=VMEM),
        scratch_shapes=[
            VMEM((512, 128), F32), VMEM((512, 128), F32), VMEM((16, 32, 128), F32), VMEM((16, 128), F32),
            VMEM((32, 16, 128), F32), dma, dma, dma((16,)), dma((16,)), dma((32,)), dma((32,)), dma((4,)), dma((4,)),
        ],
        compiler_params=pltpu.CompilerParams(collective_id=1, has_side_effects=True),
        name="gram",
    )(part)
    coef = coefficients(gall, shift_values(shift_table, shift_ids))
    step = 4
    out = sds((4, 32, 4, 16, 128), F32)
    out_spec = pl.BlockSpec((4, step, 4, 16, 128), lambda i: (0, i, 0, 0, 0))
    return pl.pallas_call(
        functools.partial(output_kernel, doms, step),
        out_shape=(out, out),
        grid=(32 // step,),
        in_specs=[
            pl.BlockSpec(memory_space=pltpu.SMEM),
            pl.BlockSpec((step, 10, 16, 128), lambda i: (i, 0, 0, 0)),
            pl.BlockSpec((2, 8, 16, 128), lambda i: (0, 0, 0, 0)),
        ],
        out_specs=(out_spec, out_spec),
        scratch_shapes=[VMEM((15, 4, 16, 128), F32)],
        compiler_params=pltpu.CompilerParams(vmem_limit_bytes=32 * MiB),
        name="outputs",
    )(coef, wide.reshape(32, 10, 16, 128), cw)


def solution(mesh):
    placed = (
        P("shift", "dom", None, None), P("dom", None, None), P("dom", None, None), P(), P("shift"),
        P(None, "dom", None, None),
    )
    return jax.shard_map(
        on_device,
        mesh=mesh,
        in_specs=placed,
        out_specs=(P("shift", None, "dom", None, None), P("shift", None, "dom", None, None)),
        check_vma=False,
    )
```

time: 180 us -> 89.7 us (0.50)
  Pallas kernels: 0 us -> 79.7 us
  blocking collectives: 57.9 us -> 0 us
  other arithmetic: 48 us -> 1.61 us
  local copies, waits for them, and re-layouts: 29.5 us -> 5.2 us
  matrix products: 18.5 us -> 1.7 us
  starting transfers between devices: 14.1 us -> 0 us
  waiting for transfers between devices: 8.8 us -> 0 us
    pallas_call x0 -> x4, Pallas kernels: none -> 79.7 us  [the longest x1 29.9 us: on_device(): pl.pallas_call(functools.partial(gram_kernel, doms, zs), out_shape=sds((4...]
    all_to_all x2 -> x0, blocking collectives: 57.9 us -> none  [the longest x1 45.2 us: sent_and_summed(): lax.all_to_all(in_blocks(array, dim, count), axis, 0, 0, tiled=True)]
    div x2 -> x0, other arithmetic: 20.3 us -> none  [the longest x1 20.3 us: on_device(): wide_w2 = (wide_z1 - center * wide_w1[:, :, 1:-1]) / 6.0]
    dot_general x2, matrix products: 18.5 us -> 1.7 us  [the longest x1 1.13 us: coefficients(): jnp.einsum('jbig,jkg->jbik', left, mix, precision=lax.Precision.HIGHEST)]
    sub x3 -> x1, other arithmetic: 13 us -> 0.01 us  [coefficients(): t = sigma - CENTER]
    slice x13 -> x1, local copies, waits for them, and re-layouts: 9.95 us -> 0.02 us  [solve_small(): h_vals = [gram[..., 1 + i, 0] for i in range(3)]]
    ppermute x4 -> x0, starting transfers between devices: 8.7 us -> none  [the longest x2 6.11 us: padded(): lax.ppermute(lax.slice_in_dim(block, block.shape[dim] - width, None, axis...]
    all_to_all x1 -> x0, waiting for transfers between devices: 8.01 us -> none  [sent_to_all(): return lax.all_to_all(copies, axis, split_axis=0, concat_axis=0, tiled=True)]
  transfers between devices with their start and end apart: 5 -> 0, of which waited for: 2 -> 0; matrix products, arithmetic and copies ran while one was open for 2% -> 0% of each run, Pallas kernels for 0% -> 0%
where the time goes in v1:
time: 89.7 us; the launch traced here: 89 us
  Pallas kernels  79.7 us (89%)
  local copies, waits for them, and re-layouts  5.2 us (6%)
  matrix products  1.7 us (2%)
  other arithmetic  1.61 us (2%)
    pallas_call x1, Pallas kernels, on_device(): pl.pallas_call(functools.partial(gram_kernel, doms, zs), out_shape=sds((4...  29.9 us
    pallas_call x1, Pallas kernels, on_device(): pl.pallas_call(functools.partial(spread_kernel, doms, zs), out_shape=(sds...  18.7 us
    pallas_call x1, Pallas kernels, on_device(): pl.pallas_call(functools.partial(output_kernel, doms, step), out_shape=(o...  16.1 us
    pallas_call x1, Pallas kernels, on_device(): pl.pallas_call(functools.partial(sketch_kernel, doms), out_shape=sds((102...  15 us
    unnamed x17, local copies, waits for them, and re-layouts  3.47 us

profile of v1, /device:TPU:0, one launch (start us, length us, event | category | flops | bytes accessed | tf_op | source)
XLA Modules:
  0.0 89.0 jit_solution(14258340072571855306)
XLA Ops:
  0.6 0.9 select_reduce_fusion
  1.5 0.1 copy.33
  1.6 0.1 copy.39
  1.7 0.1 copy.35
  1.8 0.1 stack.23
  1.9 0.1 stack.21
  2.0 0.1 stack.19
  2.1 18.7 %spread.1 = (f32[4,8,10,16,128]{4,3,2,1,0:T(8,128)}, f32[2,8,16,128]{3,2,1,0:T(8,128)}) custom-call(f32[8,4,16,128]{3,2,1,0:T(8,128)} %src.1, f32[4,16,128]{2,1,0:T(8,128)} %kap.1, f32[4,16,128]{2,1,0:T(8,128)} %mas.1), custom_call_target="tpu_custom_call" | custom-call | tf_op jit(solution)/shard_map/spread/pallas_call | solution.py:393
  20.8 1.7 %copy-done = f32[4,8,10,16,128]{4,3,2,1,0:T(8,128)S(1)} copy-done((f32[4,8,10,16,128]{4,3,2,1,0:T(8,128)S(1)}, f32[4,8,10,16,128]{4,3,2,1,0:T(8,128)}, u32[]{:S(2)}) %copy-start) | copy-done | bytes 2621464
  22.6 0.9 %copy-done.3 = f32[2,8,16,128]{3,2,1,0:T(8,128)S(1)} copy-done((f32[2,8,16,128]{3,2,1,0:T(8,128)S(1)}, f32[2,8,16,128]{3,2,1,0:T(8,128)}, u32[]{:S(2)}) %copy-start.3) | copy-done | bytes 131096
  23.5 15.0 %sketch.1.part = f32[1024,128]{1,0:T(8,128)S(1)} custom-call(bf16[1024,32,2,128]{3,2,1,0:T(2,128)(2,1)} %bitcast.42, f32[4,8,10,16,128]{4,3,2,1,0:T(8,128)S(1)} %copy-done, f32[2,8,16,128]{3,2,1,0:T(8,128)S(1)} %copy-done.3), custom_call_target="tpu_custom_call" | custom-call | tf_op jit(solution)/shard_map/sketch/pallas_call | solution.py:402
  38.5 0.8 copy-done.2
  39.3 29.9 %gram.1 = f32[4,16,128]{2,1,0:T(8,128)} custom-call(f32[1024,128]{1,0:T(8,128)} %copy-done.2), custom_call_target="tpu_custom_call" | custom-call | tf_op jit(solution)/shard_map/gram/pallas_call | solution.py:414
  69.2 0.9 reshape.831
  70.1 0.6 convolution_bitcast_fusion
  70.7 1.1 %fusion = f32[4,32,4,4]{1,3,2,0:T(4,128)S(1)} fusion(f32[4,32,4,16]{3,2,0,1:T(4,128)S(1)} %convolution_bitcast_fusion, f32[4,1,16]{2,1,0:T(1,128)S(1)} %bitcast.45, f32[4,1,16]{2,1,0:T(1,128)S(1)} %bitcast.49, f32[4,1,16]{2,1,0:T(1,128)S(1)} %bitcast.47, f32[4,1,16]{2,1,0:T(1,128)S(1)} %copy-done.5), kind=kOutput, calls=%fused_computation.1 | convolution fusion | flops 393984 | bytes 41984 | tf_op jit(solution)/shard_map/jbig,jkg->jbik/dot_general | solution.py:381
  71.9 0.1 constant_dynamic-update-slice_fusion.14
  72.1 0.1 constant_dynamic-update-slice_fusion.11
  72.2 0.1 constant_dynamic-update-slice_fusion.8
  72.3 0.1 constant_dynamic-update-slice_fusion.7
  72.4 0.1 constant_dynamic-update-slice_fusion.4
  72.7 0.1 copy.45
  72.7 0.1 reshape.833.coef
  72.9 16.1 %outputs.1 = (f32[4,32,4,16,128]{4,3,2,1,0:T(8,128)}, f32[4,32,4,16,128]{4,3,2,1,0:T(8,128)}) custom-call(f32[2048]{0:T(1024)S(1)} %reshape.833.coef, f32[32,10,16,128]{3,2,1,0:T(8,128)S(1)} %bitcast.41, f32[2,8,16,128]{3,2,1,0:T(8,128)S(1)} %copy-done.4), custom_call_target="tpu_custom_call" | custom-call | tf_op jit(solution)/shard_map/outputs/pallas_call | solution.py:430
  (31 shorter events, 0.5 us)
Async XLA Ops:
  20.8 1.7 %copy-start = (f32[4,8,10,16,128]{4,3,2,1,0:T(8,128)S(1)}, f32[4,8,10,16,128]{4,3,2,1,0:T(8,128)}, u32[]{:S(2)}) copy-start(f32[4,8,10,16,128]{4,3,2,1,0:T(8,128)} %get-tuple-element.4.wide) | copy-start | bytes 7864324
  22.6 0.9 %copy-start.3 = (f32[2,8,16,128]{3,2,1,0:T(8,128)S(1)}, f32[2,8,16,128]{3,2,1,0:T(8,128)}, u32[]{:S(2)}) copy-start(f32[2,8,16,128]{3,2,1,0:T(8,128)} %get-tuple-element.5.cw) | copy-start | bytes 393220
  23.5 46.6 %copy-start.5 = (f32[4,1,16]{2,1,0:T(1,128)S(1)}, f32[4,1,16]{2,1,0:T(1,128)}, u32[]{:S(2)}) copy-start(f32[4,1,16]{2,1,0:T(1,128)} %constant.11.clone.1) | copy-start | bytes 772
  23.5 49.4 %copy-start.1 = (f32[4,8,10,16,128]{4,3,2,1,0:T(8,128)S(1)}, f32[4,8,10,16,128]{4,3,2,1,0:T(8,128)}, u32[]{:S(2)}) copy-start(f32[4,8,10,16,128]{4,3,2,1,0:T(8,128)} %get-tuple-element.4.wide) | copy-start | bytes 7864324
  23.5 49.4 %copy-start.4 = (f32[2,8,16,128]{3,2,1,0:T(8,128)S(1)}, f32[2,8,16,128]{3,2,1,0:T(8,128)}, u32[]{:S(2)}) copy-start(f32[2,8,16,128]{3,2,1,0:T(8,128)} %get-tuple-element.5.cw) | copy-start | bytes 393220
  38.5 0.8 copy-start.2

commit v2 on v0

v2 whole, which is shorter than its diff:
```python
import functools
import jax
import jax.numpy as jnp
from jax import lax
from jax.experimental import pallas as pl
from jax.experimental.pallas import tpu as pltpu
from jax.sharding import PartitionSpec as P

F32 = jnp.float32
BF16 = jnp.bfloat16
CENTER = 2.25
K0 = 6.0 + CENTER
ORDER = (0, 1, 3, 4, 6, 7, 2, 5, 8, 9)
OWNER = (0, 1, 2, 2, 3, 3, 1, 2, 3, 3)
DEGREE = (0, 0, 0, 1, 0, 1, 1, 2, 2, 3)
LOWS = 6
VMEM = pltpu.VMEM
ANY = pl.ANY
MiB = 1024 * 1024


def rdma(src, dst, send, recv, where):
    return pltpu.make_async_remote_copy(
        src_ref=src, dst_ref=dst, send_sem=send, recv_sem=recv,
        device_id=where, device_id_type=pl.DeviceIdType.MESH,
    )


def signal(sem, where):
    pl.semaphore_signal(sem, inc=1, device_id=where, device_id_type=pl.DeviceIdType.MESH)


def neighbours(planes, i, masks):
    v = planes[i]
    first_y, last_y, first_z, last_z = masks
    beside = planes[i + 1] + planes[i - 1]
    beside = beside + jnp.where(first_y, 0.0, pltpu.roll(v, 1, 0)) + jnp.where(last_y, 0.0, pltpu.roll(v, 15, 0))
    return beside + jnp.where(first_z, 0.0, pltpu.roll(v, 1, 1)) + jnp.where(last_z, 0.0, pltpu.roll(v, 127, 1))


def make_masks():
    rows = lax.broadcasted_iota(jnp.int32, (16, 128), 0)
    lanes = lax.broadcasted_iota(jnp.int32, (16, 128), 1)
    return rows == 0, rows == 15, lanes == 0, lanes == 127


def fields_of(w, kap, mas, inside, masks):
    sixth = 1.0 / 6.0
    diag = [6.0 - kap[i] + CENTER * mas[i] for i in range(8)]

    def op(planes, i, k):
        return diag[k] * planes[i] - neighbours(planes, i, masks)

    z00, z01, p0, p1 = [], [], [], []
    for i in range(8):
        a = op(w, i + 1, i)
        b = mas[i] * w[i + 1]
        z00.append(a)
        z01.append(b)
        p0.append((a - K0 * w[i + 1]) * (sixth * inside[i]))
        p1.append((b - w[i + 1]) * sixth)
    z10, z11, z12, q0, q1, q2 = [], [], [], [], [], []
    for i in range(6):
        k = i + 1
        a = op(p0, k, k)
        b = op(p1, k, k) + mas[k] * p0[k]
        c = mas[k] * p1[k]
        z10.append(a)
        z11.append(b)
        z12.append(c)
        q0.append((a - K0 * p0[k]) * (sixth * inside[k]))
        q1.append((b - K0 * p1[k] - p0[k]) * (sixth * inside[k]))
        q2.append((c - p1[k]) * sixth)
    z20, z21, z22, z23 = [], [], [], []
    for i in range(4):
        k, n = i + 2, i + 1
        z20.append(op(q0, n, k))
        z21.append(op(q1, n, k) + mas[k] * q0[n])
        z22.append(op(q2, n, k) + mas[k] * q1[n])
        z23.append(mas[k] * q2[n])
    zs = [w[3:7], z00[2:6], z01[2:6], z10[1:5], z11[1:5], z12[1:5], z20, z21, z22, z23]
    return zs


def inside_of(d, doms):
    out = []
    for i in range(8):
        plane = d * 4 + (i - 2)
        ok = (plane >= 0) & (plane < doms * 4)
        out.append(jnp.where(ok, 1.0, 0.0).astype(F32))
    return out


def small_solve(gram, h):
    ridge = 0.001 * (gram(1, 1) + gram(2, 2) + gram(3, 3)) / 3.0 + 1.0
    e00, e11, e22 = gram(1, 1) + ridge, gram(2, 2) + ridge, gram(3, 3) + ridge
    e10, e20, e21 = gram(2, 1), gram(3, 1), gram(3, 2)
    l00 = jnp.sqrt(e00)
    l10 = e10 / l00
    l20 = e20 / l00
    l11 = jnp.sqrt(e11 - l10 * l10)
    l21 = (e21 - l20 * l10) / l11
    l22 = jnp.sqrt(e22 - l20 * l20 - l21 * l21)
    f0 = h(1) / l00
    f1 = (h(2) - l10 * f0) / l11
    f2 = (h(3) - l20 * f0 - l21 * f1) / l22
    c2 = f2 / l22
    c1 = (f1 - l21 * c2) / l11
    c0 = (f0 - l10 * c1 - l20 * c2) / l00
    return c0, c1, c2


def powers_of(t):
    return [jnp.ones_like(t), t, t * t, t * t * t]


def by_lane(shape, dim_size, values, group):
    lane = lax.broadcasted_iota(jnp.int32, shape, 1)
    which = (lane % 32) // group
    out = jnp.zeros(shape, F32)
    for j, v in enumerate(values):
        out = jnp.where(which == j, v, out)
    return out


def main_kernel(
    doms, zs, table, ids, src, kap, mas, s_ref, fields, coef,
    buf, wide, cw, fb, gb, oa, ob, part, r1, mine, r2, dm, dp, ds, rd, gall,
    loc, ssem, fsem, hs, hr, cs, cr, gs, gr, s1, e1, s2, e2, s3, e3, s4, e4, s5, e5,
):
    d, z = lax.axis_index("dom"), lax.axis_index("shift")
    up, down, far = lax.rem(z + 1, zs), lax.rem(z + zs - 1, zs), lax.rem(z + 2, zs)
    core, chip, chips = lax.rem(d, 2), d // 2, doms // 2
    partner = {"dom": d + 1 - 2 * core}
    has_l, has_r = d > 0, d < doms - 1
    copies = [
        pltpu.make_async_copy(src, wide.at[z, :, pl.ds(3, 4)], loc.at[0]),
        pltpu.make_async_copy(kap, cw.at[0, pl.ds(2, 4)], loc.at[1]),
        pltpu.make_async_copy(mas, cw.at[1, pl.ds(2, 4)], loc.at[2]),
    ]
    pairs = [pltpu.make_async_copy(s_ref.at[:, q], buf.at[q], ssem.at[q]) for q in range(32)]
    for c in copies + pairs:
        c.start()
    bar = pltpu.get_barrier_semaphore()
    for k in range(1, doms):
        signal(bar, {"dom": lax.rem(d + k, doms)})
    for k in range(1, zs):
        signal(bar, {"shift": lax.rem(z + k, zs)})

    @pl.when(d == 0)
    def _():
        for g in range(4):
            for s in range(8):
                wide[g, s, 0:3] = jnp.zeros((3, 16, 128), F32)
        cw[:, 0:2] = jnp.zeros((2, 2, 16, 128), F32)

    @pl.when(d == doms - 1)
    def _():
        for g in range(4):
            for s in range(8):
                wide[g, s, 7:10] = jnp.zeros((3, 16, 128), F32)
        cw[:, 6:8] = jnp.zeros((2, 2, 16, 128), F32)

    for c in copies:
        c.wait()
    pl.semaphore_wait(bar, doms + zs - 2)

    def to_left(g):
        return rdma(wide.at[g, :, pl.ds(3, 3)], wide.at[g, :, pl.ds(7, 3)], hs.at[0, g], hr.at[0, g], {"dom": d - 1})

    def to_right(g):
        return rdma(wide.at[g, :, pl.ds(4, 3)], wide.at[g, :, pl.ds(0, 3)], hs.at[1, g], hr.at[1, g], {"dom": d + 1})

    def coeff_left():
        return rdma(cw.at[:, pl.ds(2, 2)], cw.at[:, pl.ds(6, 2)], cs.at[0], cr.at[0], {"dom": d - 1})

    def coeff_right():
        return rdma(cw.at[:, pl.ds(4, 2)], cw.at[:, pl.ds(0, 2)], cs.at[1], cr.at[1], {"dom": d + 1})

    def start_halo(g):
        @pl.when(has_l)
        def _():
            to_left(g).start()

        @pl.when(has_r)
        def _():
            to_right(g).start()

    def wait_halo(g):
        @pl.when(has_l)
        def _():
            to_right(g).wait_recv()

        @pl.when(has_r)
        def _():
            to_left(g).wait_recv()

    @pl.when(has_l)
    def _():
        coeff_left().start()

    @pl.when(has_r)
    def _():
        coeff_right().start()

    start_halo(z)
    own = wide.at[z, :, pl.ds(3, 4)]
    send_up = rdma(own, own, gs.at[0], gr.at[0], {"shift": up})
    send_down = rdma(own, own, gs.at[1], gr.at[1], {"shift": down})
    send_up.start()
    send_down.start()

    @pl.when(has_l)
    def _():
        coeff_right().wait_recv()

    @pl.when(has_r)
    def _():
        coeff_left().wait_recv()

    wait_halo(z)
    masks = make_masks()
    inside = inside_of(d, doms)

    def fields_for(g, sketched):
        def one(s, carry):
            k = [cw[0, i] for i in range(8)]
            m = [cw[1, i] for i in range(8)]
            zf = fields_of([wide[g, s, i] for i in range(10)], k, m, inside, masks)
            at = g * 8 + s
            for n in range(10):
                for x in range(4):
                    fb[at, n, x] = zf[n][x]
            if sketched:
                col = pl.multiple_of(s * 16, 16)
                for x in range(4):
                    high = [zf[n][x] for n in ORDER]
                    low = [h - h.astype(BF16).astype(F32) for h in high[:LOWS]]
                    turned = jnp.transpose(jnp.stack(high + low, axis=0), (1, 0, 2)).astype(BF16)
                    for y in range(16):
                        gb[x * 8 + y // 2, pl.ds((y % 2) * 128 + col, 16), :] = turned[y]
            return carry

        lax.fori_loop(0, 8, one, 0)

    def save(g):
        return pltpu.make_async_copy(fb.at[pl.ds(g * 8, 8)], fields.at[pl.ds(g * 8, 8)], fsem.at[g])

    fields_for(z, True)

    send_up.wait_recv()
    half_a = wide.at[down, pl.ds(0, 4), pl.ds(3, 4)]
    relay_up = rdma(half_a, half_a, gs.at[2], gr.at[2], {"shift": up})
    relay_up.start()
    send_down.wait_recv()
    half_b = wide.at[up, pl.ds(4, 4), pl.ds(3, 4)]
    relay_down = rdma(half_b, half_b, gs.at[3], gr.at[3], {"shift": down})
    relay_down.start()
    start_halo(down)
    start_halo(up)
    for c in pairs:
        c.wait()
    save(z).start()

    rows = buf.reshape(32, 2048, 128)
    even = lax.broadcasted_iota(jnp.int32, (256, 128), 0) % 2 == 0
    other = pl.multiple_of((1 - core) * 128, 128)
    keep = pl.multiple_of(core * 128, 128)

    def swap(i):
        return rdma(part.at[i, pl.ds(other, 128)], r1.at[i], s1.at[i], e1.at[i], partner)

    def scatter(i, k):
        t = lax.rem(chip + k, chips)
        return rdma(
            mine.at[i, pl.ds(pl.multiple_of(t * 8, 8), 8)], r2.at[k, i], s2.at[k, i], e2.at[k, i], {"dom": 2 * t + core}
        )

    def spread(i):
        swap(i).wait_recv()
        mine[i] = part[i, pl.ds(keep, 128)] + r1[i]
        for k in range(1, chips):
            scatter(i, k).start()

    def stage(i, carry):
        rhs = jnp.concatenate([gb[q] for q in range(32)], axis=1)
        for base, o in ((0, oa), (1024, ob)):
            at = pl.multiple_of(i * 256 + base, 256)
            lhs = jnp.concatenate([rows[q, pl.ds(at, 256), :] for q in range(32)], axis=1)
            o[...] = lax.dot_general(lhs, rhs, (((1,), (1,)), ((), ())), preferred_element_type=F32)
        a, b = oa[...], ob[...]
        xa = a[:, :128] + pltpu.roll(a[:, 128:], 255, 0)
        xb = b[:, 128:] + pltpu.roll(b[:, :128], 1, 0)
        part[i] = jnp.where(even, xa, xb)
        swap(i).start()

        @pl.when(i > 0)
        def _():
            spread(i - 1)

        return carry

    lax.fori_loop(0, 4, stage, 0)
    relay_up.wait_recv()
    relay_down.wait_recv()
    start_halo(far)
    spread(3)
    wait_halo(down)
    fields_for(down, False)

    v = []
    for i in range(4):
        total = mine[i, pl.ds(pl.multiple_of(chip * 8, 8), 8)]
        for k in range(1, chips):
            scatter(i, k).wait_recv()
            total = total + r2[k, i]
        v.append(total)
    v = jnp.concatenate(v, axis=0)
    lane = lax.broadcasted_iota(jnp.int32, (32, 128), 1) % 16
    v = v + jnp.where(lane < LOWS, pltpu.roll(v, 118, 1), 0.0)
    v = jnp.where(lane < 10, v, 0.0)
    full = lax.dot_general(v, v, (((0,), (0,)), ((), ())), precision=lax.Precision.HIGHEST, preferred_element_type=F32)
    owner = lax.broadcasted_iota(jnp.int32, (16, 128), 1) // 16
    diag = jnp.zeros((16, 128), F32)
    for s in range(8):
        diag = jnp.where(owner == s, full[16 * s : 16 * s + 16], diag)
    dm[...] = diag
    pair = rdma(dm, dp, s3, e3, partner)
    pair.start()
    save(down).start()
    pair.wait_recv()
    ds[...] = diag + dp[...]
    sums = []
    for k in range(1, chips):
        c = rdma(ds, rd.at[k], s4.at[k], e4.at[k], {"dom": 2 * lax.rem(chip + k, chips) + core})
        c.start()
        sums.append(c)
    wait_halo(up)
    fields_for(up, False)
    total = ds[...]
    for k, c in zip(range(1, chips), sums):
        c.wait_recv()
        total = total + rd[k]
    gall[z] = total
    tail = []
    for k in range(1, zs):
        c = rdma(gall.at[z], gall.at[z], s5.at[k], e5.at[k], {"shift": lax.rem(z + k, zs)})
        c.start()
        tail.append(c)
    save(up).start()
    wait_halo(far)
    fields_for(far, False)

    shifts = [table[ids[j]] - CENTER for j in range(4)]
    r = lax.broadcasted_iota(jnp.int32, (128, 128), 0)
    l = lax.broadcasted_iota(jnp.int32, (128, 128), 1)
    tw = by_lane((128, 128), 128, shifts, 8)
    pw = powers_of(tw)
    fold = jnp.zeros((128, 128), F32)
    for n in range(10):
        hit = (r % 16 == n) & (r // 16 == l % 8) & (l // 32 == OWNER[n])
        fold = jnp.where(hit, pw[DEGREE[n]], fold)
    for c in tail:
        c.wait_recv()
    mixed = lax.dot_general(
        gall[...].reshape(64, 128), fold, (((1,), (0,)), ((), ())), precision=lax.Precision.HIGHEST, preferred_element_type=F32
    )
    save(far).start()
    t = by_lane((1, 128), 128, shifts, 8)
    pt = powers_of(t)
    lines = []
    for i in range(1, 4):
        per_z = []
        for g in range(4):
            acc = jnp.zeros((1, 128), F32)
            for n in range(10):
                if OWNER[n] == i:
                    acc = acc + pt[DEGREE[n]] * mixed[g * 16 + n : g * 16 + n + 1]
            per_z.append(acc)
        lines.append(jnp.concatenate(per_z + per_z, axis=0))

    def gram(i, k):
        return lines[i - 1] if k == 0 else pltpu.roll(lines[i - 1], 128 - 32 * k, 1)

    c0, c1, c2 = small_solve(gram, lambda i: gram(i, 0))
    t = by_lane((8, 128), 128, shifts, 8)
    center = K0 + t
    sixth = 1.0 / 6.0
    e = c1 - c2 * center * sixth
    out = [c0, c0 * t, c1, c1 * t, c1 * t * t, c2, c2 * t, c2 * t * t, c2 * t * t * t]
    out += [c0 - e * center * sixth, e * sixth, e * t * sixth, c2 * sixth, c2 * t * sixth, c2 * t * t * sixth, c2]
    quarter = lax.broadcasted_iota(jnp.int32, (8, 128), 1) // 32
    for n4 in range(4):
        acc = jnp.zeros((8, 128), F32)
        for k in range(4):
            c = out[n4 * 4 + k]
            acc = jnp.where(quarter == k, c if k == 0 else pltpu.roll(c, 32 * k, 1), acc)
        coef[n4 * 8 : n4 * 8 + 8] = acc

    for i in range(4):
        swap(i).wait_send()
        for k in range(1, chips):
            scatter(i, k).wait_send()
    for c in [pair, send_up, send_down, relay_up, relay_down] + sums + tail:
        c.wait_send()

    @pl.when(has_l)
    def _():
        coeff_left().wait_send()
        for g in range(4):
            to_left(g).wait_send()

    @pl.when(has_r)
    def _():
        coeff_right().wait_send()
        for g in range(4):
            to_right(g).wait_send()

    for g in range(4):
        save(g).wait()


def output_kernel(step, coef, fields, sol, res):
    first = pl.program_id(0) * step

    def one(b, carry):
        g, s = (first + b) // 8, lax.rem(first + b, 8)
        for j in range(4):
            c = [coef[(n // 4) * 8 + g, (n % 4) * 32 + j * 8 + s] for n in range(15)]
            for x in range(4):
                f = [fields[b, n, x] for n in range(10)]
                u = c[9] * f[0]
                for n in range(1, 6):
                    u = u + c[9 + n] * f[n]
                r = f[0] - c[0] * f[1]
                for n in range(1, 9):
                    r = r - c[n] * f[n + 1]
                sol[j, b, x] = u
                res[j, b, x] = r
        return carry

    lax.fori_loop(0, step, one, 0)


def on_device(sources, kappa, mass, shift_table, shift_ids, sketch):
    doms, zs = lax.axis_size("dom"), lax.axis_size("shift")
    sds = jax.ShapeDtypeStruct
    dma = pltpu.SemaphoreType.DMA
    smem = pl.BlockSpec(memory_space=pltpu.SMEM)
    hbm = pl.BlockSpec(memory_space=ANY)
    fields, coef = pl.pallas_call(
        functools.partial(main_kernel, doms, zs),
        out_shape=(sds((32, 10, 4, 16, 128), F32), sds((32, 128), F32)),
        in_specs=[smem, smem, hbm, hbm, hbm, hbm],
        out_specs=(hbm, pl.BlockSpec(memory_space=VMEM)),
        scratch_shapes=[
            VMEM((32, 1024, 2, 128), BF16), VMEM((4, 8, 10, 16, 128), F32), VMEM((2, 8, 16, 128), F32),
            VMEM((32, 10, 4, 16, 128), F32), VMEM((32, 256, 128), BF16), VMEM((256, 256), F32), VMEM((256, 256), F32),
            VMEM((4, 256, 128), F32), VMEM((4, 128, 128), F32), VMEM((4, 128, 128), F32), VMEM((16, 4, 8, 128), F32),
            VMEM((16, 128), F32), VMEM((16, 128), F32), VMEM((16, 128), F32), VMEM((16, 16, 128), F32), VMEM((4, 16, 128), F32),
            dma((3,)), dma((32,)), dma((4,)), dma((2, 4)), dma((2, 4)), dma((2,)), dma((2,)), dma((4,)), dma((4,)),
            dma((4,)), dma((4,)), dma((16, 4)), dma((16, 4)), dma, dma, dma((16,)), dma((16,)), dma((4,)), dma((4,)),
        ],
        compiler_params=pltpu.CompilerParams(collective_id=0, has_side_effects=True, vmem_limit_bytes=56 * MiB),
        name="main",
    )(shift_table, shift_ids, sources, kappa, mass, sketch.reshape(1024, 32, 2, 128))
    step = 4
    out = sds((4, 32, 4, 16, 128), F32)
    out_spec = pl.BlockSpec((4, step, 4, 16, 128), lambda i: (0, i, 0, 0, 0))
    return pl.pallas_call(
        functools.partial(output_kernel, step),
        out_shape=(out, out),
        grid=(32 // step,),
        in_specs=[smem, pl.BlockSpec((step, 10, 4, 16, 128), lambda i: (i, 0, 0, 0, 0))],
        out_specs=(out_spec, out_spec),
        compiler_params=pltpu.CompilerParams(vmem_limit_bytes=32 * MiB),
        name="outputs",
    )(coef, fields)


def solution(mesh):
    placed = (
        P("shift", "dom", None, None), P("dom", None, None), P("dom", None, None), P(), P("shift"),
        P(None, "dom", None, None),
    )
    return jax.shard_map(
        on_device,
        mesh=mesh,
        in_specs=placed,
        out_specs=(P("shift", None, "dom", None, None), P("shift", None, "dom", None, None)),
        check_vma=False,
    )
```

time: 180 us -> 62 us (0.34)
  blocking collectives: 57.9 us -> 0 us
  Pallas kernels: 0 us -> 55.8 us
  other arithmetic: 48 us -> 0 us
  local copies, waits for them, and re-layouts: 29.5 us -> 4.69 us
  matrix products: 18.5 us -> 0 us
  starting transfers between devices: 14.1 us -> 0 us
  waiting for transfers between devices: 8.8 us -> 0 us
    all_to_all x2 -> x0, blocking collectives: 57.9 us -> none  [the longest x1 45.2 us: sent_and_summed(): lax.all_to_all(in_blocks(array, dim, count), axis, 0, 0, tiled=True)]
    pallas_call x0 -> x2, Pallas kernels: none -> 55.8 us  [the longest x1 47.9 us: on_device(): pl.pallas_call(functools.partial(main_kernel, doms, zs), out_shape=(sds((...]
    div x4 -> x0, other arithmetic: 20.4 us -> none  [the longest x1 20.3 us: on_device(): wide_w2 = (wide_z1 - center * wide_w1[:, :, 1:-1]) / 6.0]
    dot_general x2 -> x0, matrix products: 18.5 us -> none  [the longest x1 17.5 us: project(): lax.dot_general(rows, fields, (((1,), (1,)), ((), ())), preferred_element...]
    sub x3 -> x0, other arithmetic: 13 us -> none  [the longest x1 11.6 us: on_device(): residual = w0 - c0 * z0 - c1 * z1 - c2 * z2]
    slice x13 -> x0, local copies, waits for them, and re-layouts: 9.95 us -> none  [the longest x3 3.94 us: trimmed(): inner = field[:, :, 1:-1]]
    reshape x5 -> x0, local copies, waits for them, and re-layouts: 8.97 us -> none  [the longest x3 8.8 us: flatten(): return field.astype(jnp.bfloat16).reshape(systems, -1)]
    ppermute x4 -> x0, starting transfers between devices: 8.7 us -> none  [the longest x2 6.11 us: padded(): lax.ppermute(lax.slice_in_dim(block, block.shape[dim] - width, None, axis...]
  transfers between devices with their start and end apart: 5 -> 0, of which waited for: 2 -> 0; matrix products, arithmetic and copies ran while one was open for 2% -> 0% of each run, Pallas kernels for 0% -> 0%
where the time goes in v2:
time: 62 us; the launch traced here: 61.1 us
  Pallas kernels  55.8 us (90%)
  local copies, waits for them, and re-layouts  4.69 us (8%)
  between operations  0.65 us (1%)
    pallas_call x1, Pallas kernels, on_device(): pl.pallas_call(functools.partial(main_kernel, doms, zs), out_shape=(sds((...  47.9 us
    pallas_call x1, Pallas kernels, on_device(): pl.pallas_call(functools.partial(output_kernel, step), out_shape=(out, ou...  7.91 us
    unnamed x4, local copies, waits for them, and re-layouts  4.69 us

profile of v2, /device:TPU:0, one launch (start us, length us, event | category | flops | bytes accessed | tf_op | source)
XLA Modules:
  0.0 61.1 jit_solution(2781497800077093313)
XLA Ops:
  0.6 47.9 %main.1 = (f32[32,10,4,16,128]{4,3,2,1,0:T(8,128)}, f32[32,128]{1,0:T(8,128)}) custom-call(f32[64]{0:T(128)} %table.1, s32[4]{0:T(128)} %ids.1, f32[8,4,16,128]{3,2,1,0:T(8,128)} %src.1, f32[4,16,128]{2,1,0:T(8,128)} %kap.1, f32[4,16,128]{2,1,0:T(8,128)} %mas.1, bf16[1024,32,2,128]{3,2,1,0:T(2,128)(2,1)} %bitcast.1), custom_call_target="tpu_custom_call" | custom-call | tf_op jit(solution)/shard_map/main/pallas_call | solution.py:451
  48.5 0.0 copy-start
  48.5 4.0 %copy-done = f32[32,10,4,16,128]{4,3,2,1,0:T(8,128)S(1)} copy-done((f32[32,10,4,16,128]{4,3,2,1,0:T(8,128)S(1)}, f32[32,10,4,16,128]{4,3,2,1,0:T(8,128)}, u32[]{:S(2)}) %copy-start) | copy-done | bytes 10485784
  52.5 0.0 copy-start.1
  52.5 0.7 %copy-done.1 = f32[32,128]{1,0:T(8,128)S(1)} copy-done((f32[32,128]{1,0:T(8,128)S(1)}, f32[32,128]{1,0:T(8,128)}, u32[]{:S(2)}) %copy-start.1) | copy-done | bytes 16408
  53.2 7.9 %outputs.1 = (f32[4,32,4,16,128]{4,3,2,1,0:T(8,128)}, f32[4,32,4,16,128]{4,3,2,1,0:T(8,128)}) custom-call(f32[32,128]{1,0:T(8,128)S(1)} %copy-done.1, f32[32,10,4,16,128]{4,3,2,1,0:T(8,128)S(1)} %copy-done), custom_call_target="tpu_custom_call" | custom-call | tf_op jit(solution)/shard_map/outputs/pallas_call | solution.py:470
Async XLA Ops:
  48.5 4.0 %copy-start = (f32[32,10,4,16,128]{4,3,2,1,0:T(8,128)S(1)}, f32[32,10,4,16,128]{4,3,2,1,0:T(8,128)}, u32[]{:S(2)}) copy-start(f32[32,10,4,16,128]{4,3,2,1,0:T(8,128)} %get-tuple-element.5.fields) | copy-start | bytes 31457284
  52.5 0.7 %copy-start.1 = (f32[32,128]{1,0:T(8,128)S(1)}, f32[32,128]{1,0:T(8,128)}, u32[]{:S(2)}) copy-start(f32[32,128]{1,0:T(8,128)} %get-tuple-element.4.coef) | copy-start | bytes 49156

commit v3 on v2

--- a/solution.py
+++ b/solution.py
@@ -125,7 +125,7 @@
 
 def main_kernel(
     doms, zs, table, ids, src, kap, mas, s_ref, fields, coef,
-    buf, wide, cw, fb, gb, oa, ob, part, r1, mine, r2, dm, dp, ds, rd, gall,
+    buf, wide, cw, fb, gb, ob, part, r1, mine, r2, dm, dp, ds, rd, gall,
     loc, ssem, fsem, hs, hr, cs, cr, gs, gr, s1, e1, s2, e2, s3, e3, s4, e4, s5, e5,
 ):
     d, z = lax.axis_index("dom"), lax.axis_index("shift")
@@ -165,11 +165,17 @@
         c.wait()
     pl.semaphore_wait(bar, doms + zs - 2)
 
-    def to_left(g):
-        return rdma(wide.at[g, :, pl.ds(3, 3)], wide.at[g, :, pl.ds(7, 3)], hs.at[0, g], hr.at[0, g], {"dom": d - 1})
-
-    def to_right(g):
-        return rdma(wide.at[g, :, pl.ds(4, 3)], wide.at[g, :, pl.ds(0, 3)], hs.at[1, g], hr.at[1, g], {"dom": d + 1})
+    def piece(n):
+        g = (z, z, down, up, far)[n]
+        return g, (pl.ds(4 * n, 4) if n < 2 else pl.ds(0, 8))
+
+    def to_left(n):
+        g, s = piece(n)
+        return rdma(wide.at[g, s, pl.ds(3, 3)], wide.at[g, s, pl.ds(7, 3)], hs.at[0, n], hr.at[0, n], {"dom": d - 1})
+
+    def to_right(n):
+        g, s = piece(n)
+        return rdma(wide.at[g, s, pl.ds(4, 3)], wide.at[g, s, pl.ds(0, 3)], hs.at[1, n], hr.at[1, n], {"dom": d + 1})
 
     def coeff_left():
         return rdma(cw.at[:, pl.ds(2, 2)], cw.at[:, pl.ds(6, 2)], cs.at[0], cr.at[0], {"dom": d - 1})
@@ -203,7 +209,8 @@
     def _():
         coeff_right().start()
 
-    start_halo(z)
+    start_halo(0)
+    start_halo(1)
     own = wide.at[z, :, pl.ds(3, 4)]
     send_up = rdma(own, own, gs.at[0], gr.at[0], {"shift": up})
     send_down = rdma(own, own, gs.at[1], gr.at[1], {"shift": down})
@@ -218,11 +225,11 @@
     def _():
         coeff_left().wait_recv()
 
-    wait_halo(z)
+    wait_halo(0)
     masks = make_masks()
     inside = inside_of(d, doms)
 
-    def fields_for(g, sketched):
+    def fields_for(g, sketched, begin=0, end=8):
         def one(s, carry):
             k = [cw[0, i] for i in range(8)]
             m = [cw[1, i] for i in range(8)]
@@ -241,12 +248,14 @@
                         gb[x * 8 + y // 2, pl.ds((y % 2) * 128 + col, 16), :] = turned[y]
             return carry
 
-        lax.fori_loop(0, 8, one, 0)
+        lax.fori_loop(begin, end, one, 0)
 
     def save(g):
         return pltpu.make_async_copy(fb.at[pl.ds(g * 8, 8)], fields.at[pl.ds(g * 8, 8)], fsem.at[g])
 
-    fields_for(z, True)
+    fields_for(z, True, 0, 4)
+    wait_halo(1)
+    fields_for(z, True, 4, 8)
 
     send_up.wait_recv()
     half_a = wide.at[down, pl.ds(0, 4), pl.ds(3, 4)]
@@ -256,8 +265,8 @@
     half_b = wide.at[up, pl.ds(4, 4), pl.ds(3, 4)]
     relay_down = rdma(half_b, half_b, gs.at[3], gr.at[3], {"shift": down})
     relay_down.start()
-    start_halo(down)
-    start_halo(up)
+    start_halo(2)
+    start_halo(3)
     for c in pairs:
         c.wait()
     save(z).start()
@@ -284,11 +293,12 @@
 
     def stage(i, carry):
         rhs = jnp.concatenate([gb[q] for q in range(32)], axis=1)
-        for base, o in ((0, oa), (1024, ob)):
-            at = pl.multiple_of(i * 256 + base, 256)
-            lhs = jnp.concatenate([rows[q, pl.ds(at, 256), :] for q in range(32)], axis=1)
-            o[...] = lax.dot_general(lhs, rhs, (((1,), (1,)), ((), ())), preferred_element_type=F32)
-        a, b = oa[...], ob[...]
+        at, bt = pl.multiple_of(i * 256, 256), pl.multiple_of(i * 256 + 1024, 256)
+        lhs = jnp.concatenate(
+            [jnp.concatenate([rows[q, pl.ds(at, 256), :], rows[q, pl.ds(bt, 256), :]], axis=0) for q in range(32)], axis=1
+        )
+        ob[...] = lax.dot_general(lhs, rhs, (((1,), (1,)), ((), ())), preferred_element_type=F32)
+        a, b = ob[0:256], ob[256:512]
         xa = a[:, :128] + pltpu.roll(a[:, 128:], 255, 0)
         xb = b[:, 128:] + pltpu.roll(b[:, :128], 1, 0)
         part[i] = jnp.where(even, xa, xb)
@@ -301,11 +311,11 @@
         return carry
 
     lax.fori_loop(0, 4, stage, 0)
+    spread(3)
     relay_up.wait_recv()
     relay_down.wait_recv()
-    start_halo(far)
-    spread(3)
-    wait_halo(down)
+    start_halo(4)
+    wait_halo(2)
     fields_for(down, False)
 
     v = []
@@ -335,7 +345,7 @@
         c = rdma(ds, rd.at[k], s4.at[k], e4.at[k], {"dom": 2 * lax.rem(chip + k, chips) + core})
         c.start()
         sums.append(c)
-    wait_halo(up)
+    wait_halo(3)
     fields_for(up, False)
     total = ds[...]
     for k, c in zip(range(1, chips), sums):
@@ -348,7 +358,7 @@
         c.start()
         tail.append(c)
     save(up).start()
-    wait_halo(far)
+    wait_halo(4)
     fields_for(far, False)
 
     shifts = [table[ids[j]] - CENTER for j in range(4)]
@@ -407,39 +417,69 @@
     @pl.when(has_l)
     def _():
         coeff_left().wait_send()
-        for g in range(4):
-            to_left(g).wait_send()
+        for n in range(5):
+            to_left(n).wait_send()
 
     @pl.when(has_r)
     def _():
         coeff_right().wait_send()
-        for g in range(4):
-            to_right(g).wait_send()
+        for n in range(5):
+            to_right(n).wait_send()
 
     for g in range(4):
         save(g).wait()
 
 
-def output_kernel(step, coef, fields, sol, res):
-    first = pl.program_id(0) * step
-
-    def one(b, carry):
-        g, s = (first + b) // 8, lax.rem(first + b, 8)
-        for j in range(4):
-            c = [coef[(n // 4) * 8 + g, (n % 4) * 32 + j * 8 + s] for n in range(15)]
-            for x in range(4):
-                f = [fields[b, n, x] for n in range(10)]
-                u = c[9] * f[0]
-                for n in range(1, 6):
-                    u = u + c[9 + n] * f[n]
-                r = f[0] - c[0] * f[1]
-                for n in range(1, 9):
-                    r = r - c[n] * f[n + 1]
-                sol[j, b, x] = u
-                res[j, b, x] = r
+def output_kernel(chunks, step, coef, fields, sol, res, fin, so, ro, isem, osem):
+    def take(i):
+        part = pl.ds(i * step, step)
+        return pltpu.make_async_copy(fields.at[part], fin.at[part], isem.at[i])
+
+    def put(i):
+        part = pl.ds(i * step, step)
+        return [
+            pltpu.make_async_copy(so.at[:, part], sol.at[:, part], osem.at[0, i]),
+            pltpu.make_async_copy(ro.at[:, part], res.at[:, part], osem.at[1, i]),
+        ]
+
+    for i in range(chunks):
+        take(i).start()
+
+    def chunk(i, carry):
+        take(i).wait()
+
+        def one(k, carry):
+            b = i * step + k
+            g, s = b // 8, lax.rem(b, 8)
+            for j in range(4):
+                c = [coef[(n // 4) * 8 + g, (n % 4) * 32 + j * 8 + s] for n in range(15)]
+                for x in range(4):
+                    f = [fin[b, n, x] for n in range(10)]
+                    u = c[9] * f[0]
+                    for n in range(1, 6):
+                        u = u + c[9 + n] * f[n]
+                    r = f[0] - c[0] * f[1]
+                    for n in range(1, 9):
+                        r = r - c[n] * f[n + 1]
+                    so[j, b, x] = u
+                    ro[j, b, x] = r
+            return carry
+
+        lax.fori_loop(0, step, one, 0)
+
+        @pl.when(i > 0)
+        def _():
+            for c in put(i - 1):
+                c.start()
+
         return carry
 
-    lax.fori_loop(0, step, one, 0)
+    lax.fori_loop(0, chunks, chunk, 0)
+    for c in put(chunks - 1):
+        c.start()
+    for i in range(chunks):
+        for c in put(i):
+            c.wait()
 
 
 def on_device(sources, kappa, mass, shift_table, shift_ids, sketch):
@@ -455,25 +495,27 @@
         out_specs=(hbm, pl.BlockSpec(memory_space=VMEM)),
         scratch_shapes=[
             VMEM((32, 1024, 2, 128), BF16), VMEM((4, 8, 10, 16, 128), F32), VMEM((2, 8, 16, 128), F32),
-            VMEM((32, 10, 4, 16, 128), F32), VMEM((32, 256, 128), BF16), VMEM((256, 256), F32), VMEM((256, 256), F32),
+            VMEM((32, 10, 4, 16, 128), F32), VMEM((32, 256, 128), BF16), VMEM((512, 256), F32),
             VMEM((4, 256, 128), F32), VMEM((4, 128, 128), F32), VMEM((4, 128, 128), F32), VMEM((16, 4, 8, 128), F32),
             VMEM((16, 128), F32), VMEM((16, 128), F32), VMEM((16, 128), F32), VMEM((16, 16, 128), F32), VMEM((4, 16, 128), F32),
-            dma((3,)), dma((32,)), dma((4,)), dma((2, 4)), dma((2, 4)), dma((2,)), dma((2,)), dma((4,)), dma((4,)),
+            dma((3,)), dma((32,)), dma((4,)), dma((2, 5)), dma((2, 5)), dma((2,)), dma((2,)), dma((4,)), dma((4,)),
             dma((4,)), dma((4,)), dma((16, 4)), dma((16, 4)), dma, dma, dma((16,)), dma((16,)), dma((4,)), dma((4,)),
         ],
         compiler_params=pltpu.CompilerParams(collective_id=0, has_side_effects=True, vmem_limit_bytes=56 * MiB),
         name="main",
     )(shift_table, shift_ids, sources, kappa, mass, sketch.reshape(1024, 32, 2, 128))
-    step = 4
+    step, chunks = 2, 16
     out = sds((4, 32, 4, 16, 128), F32)
-    out_spec = pl.BlockSpec((4, step, 4, 16, 128), lambda i: (0, i, 0, 0, 0))
     return pl.pallas_call(
-        functools.partial(output_kernel, step),
+        functools.partial(output_kernel, chunks, step),
         out_shape=(out, out),
-        grid=(32 // step,),
-        in_specs=[smem, pl.BlockSpec((step, 10, 4, 16, 128), lambda i: (i, 0, 0, 0, 0))],
-        out_specs=(out_spec, out_spec),
-        compiler_params=pltpu.CompilerParams(vmem_limit_bytes=32 * MiB),
+        in_specs=[smem, hbm],
+        out_specs=(hbm, hbm),
+        scratch_shapes=[
+            VMEM((32, 10, 4, 16, 128), F32), VMEM((4, 32, 4, 16, 128), F32), VMEM((4, 32, 4, 16, 128), F32),
+            dma((chunks,)), dma((2, chunks)),
+        ],
+        compiler_params=pltpu.CompilerParams(vmem_limit_bytes=60 * MiB),
         name="outputs",
     )(coef, fields)
 

time: 62 us -> 56 us (0.903); the launches traced: 61.1 us -> 55.8 us
  local copies, waits for them, and re-layouts: 4.69 us -> 0 us
    unnamed x4 -> x0, local copies, waits for them, and re-layouts: 4.69 us -> none
    pallas_call x1, Pallas kernels: 47.9 us -> 46.4 us  [on_device(): pl.pallas_call(functools.partial(main_kernel, doms, zs), out_shape=(sds((...]
    pallas_call x1, Pallas kernels: 7.91 us -> 8.75 us  [on_device(): pl.pallas_call(functools.partial(output_kernel, chunks, step), out_shape=...]
where the time goes in v3:
time: 56 us; the launch traced here: 55.8 us
  Pallas kernels  55.2 us (99%)
  between operations  0.64 us (1%)
    pallas_call x1, Pallas kernels, on_device(): pl.pallas_call(functools.partial(main_kernel, doms, zs), out_shape=(sds((...  46.4 us
    pallas_call x1, Pallas kernels, on_device(): pl.pallas_call(functools.partial(output_kernel, chunks, step), out_shape=...  8.75 us

profile of v3, /device:TPU:0, one launch (start us, length us, event | category | flops | bytes accessed | tf_op | source)
XLA Modules:
  0.0 55.8 jit_solution(12344011463878600325)
XLA Ops:
  0.6 46.4 %main.1 = (f32[32,10,4,16,128]{4,3,2,1,0:T(8,128)}, f32[32,128]{1,0:T(8,128)}) custom-call(f32[64]{0:T(128)} %table.1, s32[4]{0:T(128)} %ids.1, f32[8,4,16,128]{3,2,1,0:T(8,128)} %src.1, f32[4,16,128]{2,1,0:T(8,128)} %kap.1, f32[4,16,128]{2,1,0:T(8,128)} %mas.1, bf16[1024,32,2,128]{3,2,1,0:T(2,128)(2,1)} %bitcast.1), custom_call_target="tpu_custom_call" | custom-call | tf_op jit(solution)/shard_map/main/pallas_call | solution.py:491
  47.0 8.8 %outputs.1 = (f32[4,32,4,16,128]{4,3,2,1,0:T(8,128)}, f32[4,32,4,16,128]{4,3,2,1,0:T(8,128)}) custom-call(f32[32,128]{1,0:T(8,128)} %get-tuple-element.4.coef, f32[32,10,4,16,128]{4,3,2,1,0:T(8,128)} %get-tuple-element.5.fields), custom_call_target="tpu_custom_call" | custom-call | tf_op jit(solution)/shard_map/outputs/pallas_call | solution.py:509

commit v4 on v3

--- a/solution.py
+++ b/solution.py
@@ -124,8 +124,8 @@
 
 
 def main_kernel(
-    doms, zs, table, ids, src, kap, mas, s_ref, fields, coef,
-    buf, wide, cw, fb, gb, ob, part, r1, mine, r2, dm, dp, ds, rd, gall,
+    doms, zs, table_hbm, ids_hbm, src, kap, mas, s_ref, fields, coef,
+    table, ids, buf, wide, cw, fb, gb, ob, part, r1, mine, r2, dm, dp, ds, rd, gall,
     loc, ssem, fsem, hs, hr, cs, cr, gs, gr, s1, e1, s2, e2, s3, e3, s4, e4, s5, e5,
 ):
     d, z = lax.axis_index("dom"), lax.axis_index("shift")
@@ -138,8 +138,12 @@
         pltpu.make_async_copy(kap, cw.at[0, pl.ds(2, 4)], loc.at[1]),
         pltpu.make_async_copy(mas, cw.at[1, pl.ds(2, 4)], loc.at[2]),
     ]
+    tables = [
+        pltpu.make_async_copy(table_hbm, table, loc.at[3]),
+        pltpu.make_async_copy(ids_hbm, ids, loc.at[4]),
+    ]
     pairs = [pltpu.make_async_copy(s_ref.at[:, q], buf.at[q], ssem.at[q]) for q in range(32)]
-    for c in copies + pairs:
+    for c in copies + tables:
         c.start()
     bar = pltpu.get_barrier_semaphore()
     for k in range(1, doms):
@@ -212,6 +216,8 @@
     start_halo(0)
     start_halo(1)
     own = wide.at[z, :, pl.ds(3, 4)]
+    for c in pairs:
+        c.start()
     send_up = rdma(own, own, gs.at[0], gr.at[0], {"shift": up})
     send_down = rdma(own, own, gs.at[1], gr.at[1], {"shift": down})
     send_up.start()
@@ -267,7 +273,7 @@
     relay_down.start()
     start_halo(2)
     start_halo(3)
-    for c in pairs:
+    for c in tables + pairs:
         c.wait()
     save(z).start()
 
@@ -491,14 +497,14 @@
     fields, coef = pl.pallas_call(
         functools.partial(main_kernel, doms, zs),
         out_shape=(sds((32, 10, 4, 16, 128), F32), sds((32, 128), F32)),
-        in_specs=[smem, smem, hbm, hbm, hbm, hbm],
+        in_specs=[hbm] * 6,
         out_specs=(hbm, pl.BlockSpec(memory_space=VMEM)),
         scratch_shapes=[
-            VMEM((32, 1024, 2, 128), BF16), VMEM((4, 8, 10, 16, 128), F32), VMEM((2, 8, 16, 128), F32),
+            pltpu.SMEM((64,), F32), pltpu.SMEM((4,), jnp.int32), VMEM((32, 1024, 2, 128), BF16), VMEM((4, 8, 10, 16, 128), F32), VMEM((2, 8, 16, 128), F32),
             VMEM((32, 10, 4, 16, 128), F32), VMEM((32, 256, 128), BF16), VMEM((512, 256), F32),
             VMEM((4, 256, 128), F32), VMEM((4, 128, 128), F32), VMEM((4, 128, 128), F32), VMEM((16, 4, 8, 128), F32),
             VMEM((16, 128), F32), VMEM((16, 128), F32), VMEM((16, 128), F32), VMEM((16, 16, 128), F32), VMEM((4, 16, 128), F32),
-            dma((3,)), dma((32,)), dma((4,)), dma((2, 5)), dma((2, 5)), dma((2,)), dma((2,)), dma((4,)), dma((4,)),
+            dma((5,)), dma((32,)), dma((4,)), dma((2, 5)), dma((2, 5)), dma((2,)), dma((2,)), dma((4,)), dma((4,)),
             dma((4,)), dma((4,)), dma((16, 4)), dma((16, 4)), dma, dma, dma((16,)), dma((16,)), dma((4,)), dma((4,)),
         ],
         compiler_params=pltpu.CompilerParams(collective_id=0, has_side_effects=True, vmem_limit_bytes=56 * MiB),

time: 56 us -> 53.9 us (0.963)
  Pallas kernels: 55.2 us -> 53 us
    pallas_call x1, Pallas kernels: 46.4 us -> 44.3 us  [on_device(): pl.pallas_call(functools.partial(main_kernel, doms, zs), out_shape=(sds((...]
where the time goes in v4:
time: 53.9 us; the launch traced here: 53.7 us
  Pallas kernels  53 us (98%)
  between operations  0.64 us (1%)
    pallas_call x1, Pallas kernels, on_device(): pl.pallas_call(functools.partial(main_kernel, doms, zs), out_shape=(sds((...  44.3 us
    pallas_call x1, Pallas kernels, on_device(): pl.pallas_call(functools.partial(output_kernel, chunks, step), out_shape=...  8.75 us

profile of v4, /device:TPU:0, one launch (start us, length us, event | category | flops | bytes accessed | tf_op | source)
XLA Modules:
  0.0 53.7 jit_solution(11265509372419661918)
XLA Ops:
  0.6 44.3 %main.1 = (f32[32,10,4,16,128]{4,3,2,1,0:T(8,128)}, f32[32,128]{1,0:T(8,128)}) custom-call(f32[64]{0:T(128)} %table_hbm.1, s32[4]{0:T(128)} %ids_hbm.1, f32[8,4,16,128]{3,2,1,0:T(8,128)} %src.1, f32[4,16,128]{2,1,0:T(8,128)} %kap.1, f32[4,16,128]{2,1,0:T(8,128)} %mas.1, bf16[1024,32,2,128]{3,2,1,0:T(2,128)(2,1)} %bitcast.1), custom_call_target="tpu_custom_call" | custom-call | tf_op jit(solution)/shard_map/main/pallas_call | solution.py:497
  44.9 8.8 %outputs.1 = (f32[4,32,4,16,128]{4,3,2,1,0:T(8,128)}, f32[4,32,4,16,128]{4,3,2,1,0:T(8,128)}) custom-call(f32[32,128]{1,0:T(8,128)} %get-tuple-element.4.coef, f32[32,10,4,16,128]{4,3,2,1,0:T(8,128)} %get-tuple-element.5.fields), custom_call_target="tpu_custom_call" | custom-call | tf_op jit(solution)/shard_map/outputs/pallas_call | solution.py:515

commit v5 on v4

--- a/solution.py
+++ b/solution.py
@@ -366,6 +366,7 @@
     save(up).start()
     wait_halo(4)
     fields_for(far, False)
+    save(far).start()
 
     shifts = [table[ids[j]] - CENTER for j in range(4)]
     r = lax.broadcasted_iota(jnp.int32, (128, 128), 0)
@@ -381,7 +382,6 @@
     mixed = lax.dot_general(
         gall[...].reshape(64, 128), fold, (((1,), (0,)), ((), ())), precision=lax.Precision.HIGHEST, preferred_element_type=F32
     )
-    save(far).start()
     t = by_lane((1, 128), 128, shifts, 8)
     pt = powers_of(t)
     lines = []
@@ -436,7 +436,7 @@
         save(g).wait()
 
 
-def output_kernel(chunks, step, coef, fields, sol, res, fin, so, ro, isem, osem):
+def output_kernel(chunks, step, coef_hbm, fields, sol, res, coef, fin, so, ro, isem, osem, csem):
     def take(i):
         part = pl.ds(i * step, step)
         return pltpu.make_async_copy(fields.at[part], fin.at[part], isem.at[i])
@@ -448,11 +448,19 @@
             pltpu.make_async_copy(ro.at[:, part], res.at[:, part], osem.at[1, i]),
         ]
 
-    for i in range(chunks):
+    ahead = 4
+    first = pltpu.make_async_copy(coef_hbm, coef, csem)
+    first.start()
+    for i in range(ahead):
         take(i).start()
+    first.wait()
 
     def chunk(i, carry):
         take(i).wait()
+
+        @pl.when(i + ahead < chunks)
+        def _():
+            take(i + ahead).start()
 
         def one(k, carry):
             b = i * step + k
@@ -492,7 +500,6 @@
     doms, zs = lax.axis_size("dom"), lax.axis_size("shift")
     sds = jax.ShapeDtypeStruct
     dma = pltpu.SemaphoreType.DMA
-    smem = pl.BlockSpec(memory_space=pltpu.SMEM)
     hbm = pl.BlockSpec(memory_space=ANY)
     fields, coef = pl.pallas_call(
         functools.partial(main_kernel, doms, zs),
@@ -515,11 +522,11 @@
     return pl.pallas_call(
         functools.partial(output_kernel, chunks, step),
         out_shape=(out, out),
-        in_specs=[smem, hbm],
+        in_specs=[hbm] * 2,
         out_specs=(hbm, hbm),
         scratch_shapes=[
-            VMEM((32, 10, 4, 16, 128), F32), VMEM((4, 32, 4, 16, 128), F32), VMEM((4, 32, 4, 16, 128), F32),
-            dma((chunks,)), dma((2, chunks)),
+            pltpu.SMEM((32, 128), F32), VMEM((32, 10, 4, 16, 128), F32), VMEM((4, 32, 4, 16, 128), F32),
+            VMEM((4, 32, 4, 16, 128), F32), dma((chunks,)), dma((2, chunks)), dma,
         ],
         compiler_params=pltpu.CompilerParams(vmem_limit_bytes=60 * MiB),
         name="outputs",

time: 53.9 us -> 52.6 us (0.976)
  Pallas kernels: 53 us -> 51.7 us
    pallas_call x1, Pallas kernels: 44.3 us -> 43.3 us  [on_device(): pl.pallas_call(functools.partial(main_kernel, doms, zs), out_shape=(sds((...]
where the time goes in v5:
time: 52.6 us; the launch traced here: 52.4 us
  Pallas kernels  51.7 us (98%)
  between operations  0.64 us (1%)
    pallas_call x1, Pallas kernels, on_device(): pl.pallas_call(functools.partial(main_kernel, doms, zs), out_shape=(sds((...  43.3 us
    pallas_call x1, Pallas kernels, on_device(): pl.pallas_call(functools.partial(output_kernel, chunks, step), out_shape=...  8.38 us

profile of v5, /device:TPU:0, one launch (start us, length us, event | category | flops | bytes accessed | tf_op | source)
XLA Modules:
  0.0 52.4 jit_solution(13063830300568767691)
XLA Ops:
  0.6 43.3 %main.1 = (f32[32,10,4,16,128]{4,3,2,1,0:T(8,128)}, f32[32,128]{1,0:T(8,128)}) custom-call(f32[64]{0:T(128)} %table_hbm.1, s32[4]{0:T(128)} %ids_hbm.1, f32[8,4,16,128]{3,2,1,0:T(8,128)} %src.1, f32[4,16,128]{2,1,0:T(8,128)} %kap.1, f32[4,16,128]{2,1,0:T(8,128)} %mas.1, bf16[1024,32,2,128]{3,2,1,0:T(2,128)(2,1)} %bitcast.1), custom_call_target="tpu_custom_call" | custom-call | tf_op jit(solution)/shard_map/main/pallas_call | solution.py:504
  44.0 8.4 %outputs.1 = (f32[4,32,4,16,128]{4,3,2,1,0:T(8,128)}, f32[4,32,4,16,128]{4,3,2,1,0:T(8,128)}) custom-call(f32[32,128]{1,0:T(8,128)} %get-tuple-element.4.coef_hbm, f32[32,10,4,16,128]{4,3,2,1,0:T(8,128)} %get-tuple-element.5.fields), custom_call_target="tpu_custom_call" | custom-call | tf_op jit(solution)/shard_map/outputs/pallas_call | solution.py:522

commit v6 on v5

--- a/solution.py
+++ b/solution.py
@@ -294,7 +294,7 @@
     def spread(i):
         swap(i).wait_recv()
         mine[i] = part[i, pl.ds(keep, 128)] + r1[i]
-        for k in range(1, chips):
+        for k in (10, 2, 6, 14, 8, 9, 11, 5, 7, 13, 15, 1, 3, 4, 12):
             scatter(i, k).start()
 
     def stage(i, carry):

time: 52.6 us -> 52.2 us (level)
  no operation moved by 1% of the time
where the time goes in v6:
time: 52.2 us; the launch traced here: 51.9 us
  Pallas kernels  51.3 us (98%)
  between operations  0.64 us (1%)
    pallas_call x1, Pallas kernels, on_device(): pl.pallas_call(functools.partial(main_kernel, doms, zs), out_shape=(sds((...  42.9 us
    pallas_call x1, Pallas kernels, on_device(): pl.pallas_call(functools.partial(output_kernel, chunks, step), out_shape=...  8.38 us

profile of v6, /device:TPU:0, one launch (start us, length us, event | category | flops | bytes accessed | tf_op | source)
XLA Modules:
  0.0 51.9 jit_solution(13052794856296680449)
XLA Ops:
  0.6 42.9 %main.1 = (f32[32,10,4,16,128]{4,3,2,1,0:T(8,128)}, f32[32,128]{1,0:T(8,128)}) custom-call(f32[64]{0:T(128)} %table_hbm.1, s32[4]{0:T(128)} %ids_hbm.1, f32[8,4,16,128]{3,2,1,0:T(8,128)} %src.1, f32[4,16,128]{2,1,0:T(8,128)} %kap.1, f32[4,16,128]{2,1,0:T(8,128)} %mas.1, bf16[1024,32,2,128]{3,2,1,0:T(2,128)(2,1)} %bitcast.1), custom_call_target="tpu_custom_call" | custom-call | tf_op jit(solution)/shard_map/main/pallas_call | solution.py:504
  43.5 8.4 %outputs.1 = (f32[4,32,4,16,128]{4,3,2,1,0:T(8,128)}, f32[4,32,4,16,128]{4,3,2,1,0:T(8,128)}) custom-call(f32[32,128]{1,0:T(8,128)} %get-tuple-element.4.coef_hbm, f32[32,10,4,16,128]{4,3,2,1,0:T(8,128)} %get-tuple-element.5.fields), custom_call_target="tpu_custom_call" | custom-call | tf_op jit(solution)/shard_map/outputs/pallas_call | solution.py:522
